TPU v7x, 128 devices: a whole 4x4x4 slice. The times are simulated.
128 devices in a mesh: grp: 4 (over x), tile: 32 (over y, z, core).
Axes of the slice: x: 4, y: 4, z: 4, core: 2. Of those that a mesh axis runs over, the one named last changes fastest.
Arguments:
- descriptors: bfloat16 [64, 4096, 256], P('grp', 'tile'), may hold values from -8 to 8
- pairs: int32 [32, 2], P('grp'), may hold values from 0 to 63, as said below
- counts: int32 [64], replicated, may hold values from 1024 to 4096
Outputs:
- row_lse: float32 [32, 4096], P('grp', 'tile')
- col_lse: float32 [32, 4096], P('grp', 'tile')
- best_log: float32 [32, 4096], P('grp', 'tile')
Inputs may be any that keep to these rules, and one draw needn't show every extreme that they name: `pairs`: the two images of a pair differ.
All inputs are finite; a program needn't handle non-finite values.
Results may differ from a plain program's by a relative error of at most 0.0003.
Values may be sent and summed in bfloat16 or wider, within the bound.
A program may use at most 64 MiB of HBM per device.

v0:
```python
import math

import jax
import jax.numpy as jnp
from jax import lax
from jax.sharding import Mesh
from jax.sharding import PartitionSpec as P

QBLK = 4
TILE = ("tile_0", "tile_1", "tile_2")


NEGATIVE = -1e30


def in_one_piece(arrays, axis, split_dim, concat_dim, along):
    both = jnp.concatenate(arrays, axis=along)
    out, at, outs = (
        lax.all_to_all(both, axis, split_axis=split_dim, concat_axis=concat_dim, tiled=True),
        0,
        [],
    )
    for a in arrays:
        outs.append(lax.slice_in_dim(out, at, at + a.shape[along], axis=along))
        at += a.shape[along]
    return tuple(outs)


def in_blocks(value, dim, count):
    lengths = value.shape
    tiles = value.reshape(*lengths[:dim], count, lengths[dim] // count, *lengths[dim + 1 :])
    return jnp.moveaxis(tiles, dim, 0)


def joined_along(tiles, dim):
    lengths = list(tiles.shape[1:])
    lengths[dim] *= tiles.shape[0]
    return jnp.moveaxis(tiles, 0, dim).reshape(lengths)


def exchange_in_order(tiles, axes, turns):
    inside = tiles.shape[1:]
    out = tiles.reshape(*(lax.axis_size(a) for a in axes), *inside)
    for k in turns:
        out = lax.all_to_all(out, axes[k], k, k, tiled=True)
    return out.reshape(-1, *inside)


def core_and_chips(value, groups, turns, split_dim, concat_dim):
    count = lax.axis_size(groups[0]) * lax.axis_size(groups[1])
    tiles = in_blocks(value, split_dim, count)
    return joined_along(exchange_in_order(tiles, groups, turns), concat_dim)


def join_stats(earlier, later):
    highest = jnp.maximum(earlier[0], later[0])
    summed = earlier[1] * jnp.exp(earlier[0] - highest) + later[1] * jnp.exp(later[0] - highest)
    return (highest, summed)


def slot_first(item, query_index, score_scale):
    query_rows, key_image, query_count, key_count = item
    height = query_rows.shape[0]
    width = query_rows.shape[1]
    total_keys = key_image.shape[0]
    block = min(512, height)
    number = height // block
    key_mask = (lax.iota(jnp.int32, total_keys) < key_count)[None, :]
    grouped = query_rows.reshape(number, block, width)
    index_groups = query_index.reshape(number, block)

    def first_pass(carried, inputs):
        block_rows, block_index = inputs
        scores = (
            jnp.einsum("qd,kd->qk", block_rows, key_image, preferred_element_type=jnp.float32)
            * score_scale
        )
        query_mask = (block_index < query_count)[:, None]
        row_top = jnp.max(jnp.where(key_mask, scores, NEGATIVE), axis=1)
        row_total = jnp.sum(jnp.where(key_mask, jnp.exp(scores - row_top[:, None]), 0.0), axis=1)
        col_top = jnp.max(jnp.where(query_mask, scores, NEGATIVE), axis=0)
        col_total = jnp.sum(jnp.where(query_mask, jnp.exp(scores - col_top[None, :]), 0.0), axis=0)
        return (join_stats(carried, (col_top, col_total)), row_top + jnp.log(row_total))

    start_stats = (
        jnp.full((total_keys,), NEGATIVE, jnp.float32),
        jnp.zeros((total_keys,), jnp.float32),
    )
    col_stats, row_values = lax.scan(first_pass, start_stats, (grouped, index_groups))
    return (col_stats[0], col_stats[1], row_values.reshape(height))


def slot_second(item, query_index, score_scale):
    query_rows, key_image, row_values, col_values, query_count, key_count = item
    height = query_rows.shape[0]
    width = query_rows.shape[1]
    total_keys = key_image.shape[0]
    block = min(512, height)
    number = height // block
    key_mask = (lax.iota(jnp.int32, total_keys) < key_count)[None, :]
    grouped = query_rows.reshape(number, block, width)
    lse_groups = row_values.reshape(number, block)

    def second_pass(carried, inputs):
        block_rows, block_lse = inputs
        scores = (
            jnp.einsum("qd,kd->qk", block_rows, key_image, preferred_element_type=jnp.float32)
            * score_scale
        )
        best = (
            jnp.max(jnp.where(key_mask, 2.0 * scores - col_values[None, :], NEGATIVE), axis=1)
            - block_lse
        )
        return (carried, best)

    unused, best_values = lax.scan(second_pass, jnp.int32(0), (grouped, lse_groups))
    query_valid = query_index < query_count
    return (
        jnp.where(query_valid, row_values, 0.0),
        jnp.where(query_valid, best_values.reshape(height), 0.0),
    )


def paired_blocks(queries, keys_local, query_counts, key_counts, score_scale):
    devices_here = lax.axis_size(TILE)
    rows = queries.shape[1]
    width = queries.shape[2]
    slots = devices_here // QBLK
    sub = rows // QBLK
    pair_count = queries.shape[0]
    per_slot = -(-pair_count // slots)
    padded = per_slot * slots
    query_send = (
        queries.reshape(slots, per_slot, QBLK, sub, width)
        .transpose(0, 2, 1, 3, 4)
        .reshape(devices_here, per_slot, sub, width)
    )
    key_send = jnp.broadcast_to(
        keys_local.reshape(slots, 1, per_slot, rows, width), (slots, QBLK, per_slot, rows, width)
    ).reshape(devices_here, per_slot, rows, width)
    query_got, key_got = in_one_piece((query_send, key_send), TILE, 0, 0, 2)
    query_here = query_got.transpose(1, 0, 2, 3).reshape(per_slot, devices_here * sub, width)
    key_here = key_got.transpose(1, 0, 2, 3).reshape(per_slot, devices_here * rows, width)
    place = lax.axis_index(TILE)
    slot = place // QBLK
    quarter = place % QBLK
    query_index = (
        lax.iota(jnp.int32, devices_here)[:, None] * rows
        + quarter * sub
        + lax.iota(jnp.int32, sub)[None, :]
    ).reshape(devices_here * sub)
    query_own = lax.dynamic_slice_in_dim(query_counts, slot * per_slot, per_slot, 0)
    key_own = lax.dynamic_slice_in_dim(key_counts, slot * per_slot, per_slot, 0)
    col_top, col_total, row_values = lax.map(
        lambda item: slot_first(item, query_index, score_scale),
        (query_here, key_here, query_own, key_own),
    )

    def by_block(values):
        return values.reshape(per_slot, devices_here, rows).transpose(1, 0, 2)

    top_got, total_got = in_one_piece((by_block(col_top), by_block(col_total)), TILE, 0, 0, 1)
    top_got = top_got.reshape(slots, QBLK, per_slot, rows)
    total_got = total_got.reshape(slots, QBLK, per_slot, rows)
    stats = (top_got[:, 0], total_got[:, 0])
    for member in range(1, QBLK):
        stats = join_stats(stats, (top_got[:, member], total_got[:, member]))
    col_block = stats[0] + jnp.log(stats[1])
    col_send = jnp.broadcast_to(col_block[:, None], (slots, QBLK, per_slot, rows)).reshape(
        devices_here, per_slot, rows
    )
    col_got = core_and_chips(col_send, (("tile_0", "tile_1"), "tile_2"), (1, 0), 0, 0)
    col_values = col_got.transpose(1, 0, 2).reshape(per_slot, devices_here * rows)
    row_out, best_out = lax.map(
        lambda item: slot_second(item, query_index, score_scale),
        (query_here, key_here, row_values, col_values, query_own, key_own),
    )

    def to_owner(values):
        return values.reshape(per_slot, devices_here, sub).transpose(1, 0, 2)

    row_got, best_got = (
        lax.all_to_all(to_owner(row_out), TILE, split_axis=0, concat_axis=0, tiled=True),
        lax.all_to_all(to_owner(best_out), TILE, split_axis=0, concat_axis=0, tiled=True),
    )

    def from_slots(values):
        return (
            values.reshape(slots, QBLK, per_slot, sub).transpose(0, 2, 1, 3).reshape(padded, rows)
        )

    key_place = place * rows + lax.iota(jnp.int32, rows)
    key_valid_own = key_place[None, :] < key_counts[:, None]
    col_out = jnp.where(key_valid_own, col_block.reshape(padded, rows), 0.0)
    return (from_slots(row_got), col_out, from_slots(best_got))


def local(descriptors, pairs, counts):
    score_scale = 2.0 / math.sqrt(descriptors.shape[2])
    image_rows = lax.all_gather(descriptors, "grp", axis=0, tiled=True)
    image_ids = lax.iota(jnp.int32, counts.shape[0])
    first_image = pairs[:, 0]
    second = pairs[:, 1]
    query_counts = jnp.sum(
        jnp.where(first_image[:, None] == image_ids[None, :], counts[None, :], 0), axis=1
    )
    key_counts = jnp.sum(
        jnp.where(second[:, None] == image_ids[None, :], counts[None, :], 0), axis=1
    )
    queries = jnp.take(image_rows, first_image, axis=0)
    keys_local = jnp.take(image_rows, second, axis=0)
    return paired_blocks(queries, keys_local, query_counts, key_counts, score_scale)


def solution(mesh):
    torus = Mesh(
        mesh.devices.reshape(mesh.shape["grp"], 4, 4, 2), ("grp", "tile_0", "tile_1", "tile_2")
    )
    return jax.shard_map(
        local,
        mesh=torus,
        in_specs=(P("grp", TILE, None), P("grp", None), P()),
        out_specs=(P("grp", TILE), P("grp", TILE), P("grp", TILE)),
        check_vma=False,
    )
```

profile of v0, /device:TPU:1, one launch (start us, length us, event | category | flops | bytes accessed | tf_op | source)
XLA Modules:
  0.0 198.5 jit_solution(10425971025592148428)
XLA Ops:
  8.7 52.2 %all-gather.2.cloned.1.call-done = bf16[64,128,256]{2,1,0:T(8,128)(2,1)} async-done(((bf16[16,128,256]{2,1,0:T(8,128)(2,1)}), bf16[64,128,256]{2,1,0:T(8,128)(2,1)}) %all-gather.2.cloned.1.call-update) | async-done | bytes 4194320 | tf_op jit(solution)/shard_map/all_gather | solution.py:200
  60.9 2.8 %gather_fusion = bf16[8,128,256]{2,1,0:T(8,128)(2,1)S(1)} fusion(bf16[64,128,256]{2,1,0:T(8,128)(2,1)} %all-gather.2.cloned.1.call-done, s32[1024]{0:T(1024)S(1)} %pad_clamp_fusion.1), kind=kCustom, calls=%fused_computation.clone | custom fusion | bytes 1048608 | tf_op jit(solution)/shard_map/jit(_take)/gather | solution.py:210
  63.7 2.8 %gather_fusion.1 = bf16[8,128,256]{2,1,0:T(8,128)(2,1)S(1)} fusion(bf16[64,128,256]{2,1,0:T(8,128)(2,1)} %all-gather.2.cloned.1.call-done, s32[1024]{0:T(1024)S(1)} %pad_clamp_fusion), kind=kCustom, calls=%fused_computation.1.clone | custom fusion | bytes 1048608 | tf_op jit(solution)/shard_map/jit(_take)/gather | solution.py:211
  66.9 1.7 pad_maximum_fusion
  68.6 7.9 %all-to-all-start = ((bf16[32,1,160,256]{3,2,1,0:T(8,128)(2,1)}), bf16[32,1,160,256]{3,2,1,0:T(8,128)(2,1)S(1)}, u32[]{:S(2)}, u32[]{:S(2)}) async-start(bf16[32,1,160,256]{3,2,1,0:T(8,128)(2,1)} %pad_maximum_fusion), calls=%async_computation | async-start | bytes 5242880 | tf_op jit(solution)/shard_map/all_to_all | solution.py:19
  78.2 32.2 %all-to-all-done = bf16[32,1,160,256]{3,2,1,0:T(8,128)(2,1)S(1)} async-done(((bf16[32,1,160,256]{3,2,1,0:T(8,128)(2,1)}), bf16[32,1,160,256]{3,2,1,0:T(8,128)(2,1)S(1)}, u32[]{:S(2)}, u32[]{:S(2)}) %all-to-all-start) | async-done | bytes 2621472 | tf_op jit(solution)/shard_map/all_to_all | solution.py:19
  110.4 1.5 slice.61
  112.0 20.6 %while.48 = (s32[]{:T(128)}, f32[4096]{0:T(1024)S(1)}, f32[4096]{0:T(1024)S(1)}, f32[2,512]{1,0:T(2,128)S(1)}, s32[2,512]{1,0:T(2,128)S(1)}, /*index=5*/s32[]{:T...) while((s32[]{:T(128)}, f32[4096]{0:T(1024)S(1)}, ...), condition=%wide.region_7.9_spmd.clone, body=%wide.region_2.8_spmd.clone.sunk | while | flops 1098936320 | bytes 19316360 | solution.py:89
  113.3 4.0 %select_reduce_fusion.11 = (f32[512]{0:T(512)S(1)}, f32[4096]{0:T(1024)S(1)}, f32[512,4096]{1,0:T(8,128)S(1)}) fusion(pred[4096]{0:T(1024)(128)(4,1)S(1)} %compare_reduce_fusion.7, pred[512]{0:T(512)(128)(4,1)S(1)} %compare_reduce_fusion.8, bf16[4096,256]{1,0:T(8,128)(2,1)} %get-tuple-element.457, bf16[2,512,256]{2,1,0:T(8,128)(2,1)S(1)} %get-tuple-element.456, ...), kind=kOutput, calls=%fused_computation.11.clone.1 | convolution fusion | flops 1084222976 | bytes 10770948 | tf_op jit(solution)/shard_map/while/body/eval_jaxpr/while/body/eval_jaxpr/qd,kd->qk/dot_general | solution.py:75
  117.3 4.8 %select_reduce_fusion.12 = (f32[512]{0:T(512)S(1)}, f32[4096]{0:T(1024)S(1)}) fusion(f32[512,4096]{1,0:T(8,128)S(1)} %get-tuple-element.421, f32[512]{0:T(512)S(1)} %get-tuple-element.422, pred[4096]{0:T(1024)(128)(4,1)S(1)} %compare_reduce_fusion.7, f32[4096]{0:T(1024)S(1)} %get-tuple-element.423, pred[512]{0:T(512)(128)(4,1)S(1)} %compare_reduce_fusion.8), kind=kLoop, calls=%fused_computation.10.clone.1 | loop fusion | flops 14675456 | bytes 8430080 | tf_op jit(solution)/shard_map/while/body/eval_jaxpr/while/body/eval_jaxpr/reduce_sum | solution.py:80
  123.6 3.9 %select_reduce_fusion.11 = (f32[512]{0:T(512)S(1)}, f32[4096]{0:T(1024)S(1)}, f32[512,4096]{1,0:T(8,128)S(1)}) fusion(pred[4096]{0:T(1024)(128)(4,1)S(1)} %compare_reduce_fusion.7, pred[512]{0:T(512)(128)(4,1)S(1)} %compare_reduce_fusion.8, bf16[4096,256]{1,0:T(8,128)(2,1)} %get-tuple-element.457, bf16[2,512,256]{2,1,0:T(8,128)(2,1)S(1)} %get-tuple-element.456, ...), kind=kOutput, calls=%fused_computation.11.clone.1 | convolution fusion | flops 1084222976 | bytes 10770948 | tf_op jit(solution)/shard_map/while/body/eval_jaxpr/while/body/eval_jaxpr/qd,kd->qk/dot_general | solution.py:75
  127.6 4.8 %select_reduce_fusion.12 = (f32[512]{0:T(512)S(1)}, f32[4096]{0:T(1024)S(1)}) fusion(f32[512,4096]{1,0:T(8,128)S(1)} %get-tuple-element.421, f32[512]{0:T(512)S(1)} %get-tuple-element.422, pred[4096]{0:T(1024)(128)(4,1)S(1)} %compare_reduce_fusion.7, f32[4096]{0:T(1024)S(1)} %get-tuple-element.423, pred[512]{0:T(512)(128)(4,1)S(1)} %compare_reduce_fusion.8), kind=kLoop, calls=%fused_computation.10.clone.1 | loop fusion | flops 14675456 | bytes 8430080 | tf_op jit(solution)/shard_map/while/body/eval_jaxpr/while/body/eval_jaxpr/reduce_sum | solution.py:80
  132.6 11.1 %all_to_all.30 = f32[32,2,128]{2,1,0:T(2,128)S(1)} all-to-all(f32[32,2,128]{2,1,0:T(2,128)S(1)} %pad_maximum_fusion.1), channel_id=1, replica_groups=mesh['grp'=4,'tile_0'=4,'tile_1'=4,'tile_2'=2] {'tile_0','tile_1','tile_2'}, dimensions={0} | all-to-all | bytes 65536 | tf_op jit(solution)/shard_map/all_to_all | solution.py:19
  143.8 3.8 %all_to_all.31 = f32[16,2,1,1,128]{4,3,2,0,1:T(1,128)S(1)} all-to-all(f32[16,2,1,1,128]{4,3,2,0,1:T(1,128)S(1)} %broadcast_in_dim.147), channel_id=1, replica_groups=mesh['grp'=4,'tile_0'=4,'tile_1'=4,'tile_2'=2] {'tile_2'}, dimensions={1} | all-to-all | bytes 32768 | tf_op jit(solution)/shard_map/all_to_all | solution.py:45
  148.1 3.5 %all-to-all-start.4 = ((f32[16,2,1,1,128]{4,3,2,1,0:T(1,128)}), f32[16,2,1,1,128]{4,3,2,1,0:T(1,128)S(1)}, u32[]{:S(2)}, u32[]{:S(2)}) async-start(f32[16,2,1,1,128]{4,3,2,1,0:T(1,128)} %copy.107), calls=%async_computation.4 | async-start | bytes 32768 | tf_op jit(solution)/shard_map/all_to_all | solution.py:45
  151.8 6.3 %all-to-all-done.4 = f32[16,2,1,1,128]{4,3,2,1,0:T(1,128)S(1)} async-done(((f32[16,2,1,1,128]{4,3,2,1,0:T(1,128)}), f32[16,2,1,1,128]{4,3,2,1,0:T(1,128)S(1)}, u32[]{:S(2)}, u32[]{:S(2)}) %all-to-all-start.4) | async-done | bytes 16416 | tf_op jit(solution)/shard_map/all_to_all | solution.py:45
  158.0 7.6 %while.47 = (s32[]{:T(128)}, f32[2,512]{1,0:T(2,128)S(1)}, bf16[2,512,256]{2,1,0:T(8,128)(2,1)S(1)}, bf16[4096,256]{1,0:T(8,128)(2,1)}, f32[4096]{0:T(1024)S(1)}...) while((s32[]{:T(128)}, f32[2,512]{1,0:T(2,128)S(1)}, ...), condition=%wide.region_10.12_spmd.clone, body=%wide.region_8.11_spmd.clone.sunk | while | flops 1082134528 | bytes 2396269 | solution.py:116
  158.7 3.0 %select_reduce_fusion.10 = f32[512]{0:T(512)S(1)} fusion(bf16[4096,256]{1,0:T(8,128)(2,1)} %get-tuple-element.482, f32[4096]{0:T(1024)S(1)} %get-tuple-element.483, pred[4096]{0:T(1024)(128)(4,1)S(1)} %compare_reduce_fusion.6, bf16[2,512,256]{2,1,0:T(8,128)(2,1)S(1)} %get-tuple-element.481, s32[]{:T(128)} %get-tuple-element.470), kind=kOutput, calls=%fused_computation.4.clone.1 | convolution fusion | flops 1082129920 | bytes 2381828 | tf_op jit(solution)/shard_map/while/body/eval_jaxpr/while/body/eval_jaxpr/qd,kd->qk/dot_general | solution.py:107
  162.5 3.0 %select_reduce_fusion.10 = f32[512]{0:T(512)S(1)} fusion(bf16[4096,256]{1,0:T(8,128)(2,1)} %get-tuple-element.482, f32[4096]{0:T(1024)S(1)} %get-tuple-element.483, pred[4096]{0:T(1024)(128)(4,1)S(1)} %compare_reduce_fusion.6, bf16[2,512,256]{2,1,0:T(8,128)(2,1)S(1)} %get-tuple-element.481, s32[]{:T(128)} %get-tuple-element.470), kind=kOutput, calls=%fused_computation.4.clone.1 | convolution fusion | flops 1082129920 | bytes 2381828 | tf_op jit(solution)/shard_map/while/body/eval_jaxpr/while/body/eval_jaxpr/qd,kd->qk/dot_general | solution.py:107
  165.7 1.4 compare_select_fusion
  167.1 4.9 %all-to-all-start.1 = ((f32[32,1,32]{2,1,0:T(1,128)}), f32[32,1,32]{2,1,0:T(1,128)S(1)}, u32[]{:S(2)}, u32[]{:S(2)}) async-start(f32[32,1,32]{2,1,0:T(1,128)} %get-tuple-element.313), calls=%async_computation.1 | async-start | bytes 32768 | tf_op jit(solution)/shard_map/all_to_all | solution.py:183
  172.0 7.1 %all-to-all-done.1 = f32[32,1,32]{2,1,0:T(1,128)S(1)} async-done(((f32[32,1,32]{2,1,0:T(1,128)}), f32[32,1,32]{2,1,0:T(1,128)S(1)}, u32[]{:S(2)}, u32[]{:S(2)}) %all-to-all-start.1) | async-done | bytes 4128 | tf_op jit(solution)/shard_map/all_to_all | solution.py:183
  179.1 4.2 %all-to-all-start.5 = ((f32[32,1,32]{2,1,0:T(1,128)}), f32[32,1,32]{2,1,0:T(1,128)S(1)}, u32[]{:S(2)}, u32[]{:S(2)}) async-start(f32[32,1,32]{2,1,0:T(1,128)} %get-tuple-element.312), calls=%async_computation.5 | async-start | bytes 32768 | tf_op jit(solution)/shard_map/all_to_all | solution.py:184
  185.8 4.5 %all-to-all-done.5 = f32[32,1,32]{2,1,0:T(1,128)S(1)} async-done(((f32[32,1,32]{2,1,0:T(1,128)}), f32[32,1,32]{2,1,0:T(1,128)S(1)}, u32[]{:S(2)}, u32[]{:S(2)}) %all-to-all-start.5) | async-done | bytes 4128 | tf_op jit(solution)/shard_map/all_to_all | solution.py:184
  (60 shorter events, 12.8 us)
Async XLA Ops:
  7.2 53.7 %all-gather.2.cloned.1.call-start = ((), (), s32[]{:S(2)}) async-start(), calls=%async_computation.6 | async-start | bytes 5242880 | tf_op jit(solution)/shard_map/all_gather | solution.py:200
  63.6 12.9 %copy-start = (s32[8,2]{0,1:T(2,128)S(1)}, s32[8,2]{0,1:T(2,128)}, u32[]{:S(2)}) copy-start(s32[8,2]{0,1:T(2,128)} %param.10) | copy-start | bytes 196
  63.7 12.9 %copy-start.1 = (s32[64]{0:T(128)S(1)}, s32[64]{0:T(128)}, u32[]{:S(2)}) copy-start(s32[64]{0:T(128)} %param.11) | copy-start | bytes 772
  68.6 41.8 %all-to-all-start = ((bf16[32,1,160,256]{3,2,1,0:T(8,128)(2,1)}), bf16[32,1,160,256]{3,2,1,0:T(8,128)(2,1)S(1)}, u32[]{:S(2)}, u32[]{:S(2)}) async-start(bf16[32,1,160,256]{3,2,1,0:T(8,128)(2,1)} %pad_maximum_fusion), calls=%async_computation | async-start | bytes 5242880 | tf_op jit(solution)/shard_map/all_to_all | solution.py:19
  148.1 9.9 %all-to-all-start.4 = ((f32[16,2,1,1,128]{4,3,2,1,0:T(1,128)}), f32[16,2,1,1,128]{4,3,2,1,0:T(1,128)S(1)}, u32[]{:S(2)}, u32[]{:S(2)}) async-start(f32[16,2,1,1,128]{4,3,2,1,0:T(1,128)} %copy.107), calls=%async_computation.4 | async-start | bytes 32768 | tf_op jit(solution)/shard_map/all_to_all | solution.py:45
  167.1 12.0 %all-to-all-start.1 = ((f32[32,1,32]{2,1,0:T(1,128)}), f32[32,1,32]{2,1,0:T(1,128)S(1)}, u32[]{:S(2)}, u32[]{:S(2)}) async-start(f32[32,1,32]{2,1,0:T(1,128)} %get-tuple-element.313), calls=%async_computation.1 | async-start | bytes 32768 | tf_op jit(solution)/shard_map/all_to_all | solution.py:183
  179.1 11.2 %all-to-all-start.5 = ((f32[32,1,32]{2,1,0:T(1,128)}), f32[32,1,32]{2,1,0:T(1,128)S(1)}, u32[]{:S(2)}, u32[]{:S(2)}) async-start(f32[32,1,32]{2,1,0:T(1,128)} %get-tuple-element.312), calls=%async_computation.5 | async-start | bytes 32768 | tf_op jit(solution)/shard_map/all_to_all | solution.py:184
Sparse Core Ops, SparseCore 0:
  9.6 51.1 all-gather.1
where the time goes:
time: 199 us
  waiting for transfers between devices  103 us (52%)
  starting transfers between devices  20.5 us (10%)
  other arithmetic  20.3 us (10%)
  blocking collectives  14.8 us (7%)
  between operations  14.3 us (7%)
  matrix products  13.9 us (7%)
  local copies, waits for them, and re-layouts  11.7 us (6%)
    all_gather x1, waiting for transfers between devices, local(): image_rows = lax.all_gather(descriptors, 'grp', axis=0, tiled=True)  52.2 us
    all_to_all x1, waiting for transfers between devices, in_one_piece(): lax.all_to_all(both, axis, split_axis=split_dim, concat_axis=concat_dim,...  32.2 us
    all_to_all x1, blocking collectives, in_one_piece(): lax.all_to_all(both, axis, split_axis=split_dim, concat_axis=concat_dim,...  11.1 us
    reduce_sum x2, other arithmetic, first_pass(): jnp.sum(jnp.where(key_mask, jnp.exp(scores - row_top[:, None]), 0.0), axi...  9.7 us
    dot_general x2, matrix products, first_pass(): jnp.einsum('qd,kd->qk', block_rows, key_image, preferred_element_type=jnp...  7.9 us
    all_to_all x1, starting transfers between devices, in_one_piece(): lax.all_to_all(both, axis, split_axis=split_dim, concat_axis=concat_dim,...  7.87 us
    all_to_all x1, waiting for transfers between devices, paired_blocks(): lax.all_to_all(to_owner(row_out), TILE, split_axis=0, concat_axis=0, tile...  7.06 us
    all_to_all x1, waiting for transfers between devices, exchange_in_order(): out = lax.all_to_all(out, axes[k], k, k, tiled=True)  6.28 us
  transfers between devices with their start and end apart: 5, of which 5 were waited for; matrix products, arithmetic and copies ran while one was open for 3% of the time, Pallas kernels for 0%

commit v1 on v0

v1 whole, which is shorter than its diff:
```python
import functools
import math

import jax
import jax.numpy as jnp
from jax import lax
from jax.experimental import pallas as pl
from jax.experimental.pallas import tpu as pltpu
from jax.sharding import Mesh
from jax.sharding import PartitionSpec as P

TILE = ("tile_0", "tile_1", "tile_2")
MESH = pl.DeviceIdType.MESH

NEGATIVE = -1e30
CHUNKS = 8
ROWS = 16
GROUPS = 4
IMAGES = 16
SOURCES = 8
MEMBERS = 4
LOG2E = math.log2(math.e)
LN2 = math.log(2.0)


def slot_index(z, core, chunk, lane):
    outer = jnp.logical_or(z == 0, z == 3)
    low = jnp.where(outer, 0, 1)
    high = jnp.where(outer, 3, 2)
    source = lane // ROWS
    z_source = jnp.where(source % 2 == 0, low, high)
    tile = (source // 2) * 8 + z_source * 2 + core
    return tile * (CHUNKS * ROWS) + chunk * ROWS + lane % ROWS


def block_transpose(x):
    sub = lax.broadcasted_iota(jnp.int32, (8, 128), 0)
    block = lax.broadcasted_iota(jnp.int32, (8, 128), 1) // ROWS
    out = x
    for d in range(8):
        moved = x if d == 0 else pltpu.roll(pltpu.roll(x, ROWS * d, 1), 8 - d, 0)
        out = jnp.where(block == (sub + d) % 8, moved, out)
    return out


def kernel(scale, pairs, counts, desc, out_row, out_col, out_best, *scratch):
    gathered = scratch[:CHUNKS]
    staged = scratch[CHUNKS : 2 * CHUNKS]
    (
        queries, keys, scores, row_top, row_sum, col_top, col_sum, key_bias, query_bias,
        stats, stats_got, col_full, best_cols, sent, got,
        load_sem, xs, xr, qs, qr, ks, kr, fs, fr, cs, cr, vs, vr, os_, or_,
    ) = scratch[2 * CHUNKS :]
    x, y, z, c = (lax.axis_index(a) for a in ("grp",) + TILE)
    right = (lax.rem(x + 1, 4), y, z, c)
    left = (lax.rem(x + 3, 4), y, z, c)
    half = z // 2
    parity = z % 2
    place = y * 2 + half
    member = parity * 2 + c
    z_beside = half * 2 + (1 - parity)
    beside = (x, y, z_beside, c)
    sibling = (x, y, z, 1 - c)
    diagonal = (x, y, z_beside, 1 - c)
    member_beside = (1 - parity) * 2 + c

    def peer(dy, dk):
        return (x, lax.rem(y + dy, 4), z if dk == 0 else 3 - z, c)

    def peer_place(dy, dk):
        return lax.rem(y + dy, 4) * 2 + (half if dk == 0 else 1 - half)

    loads = [
        pltpu.make_async_copy(
            desc.at[:, pl.ds(r * ROWS, ROWS), :], gathered[r].at[pl.ds(0, IMAGES)], load_sem.at[r]
        )
        for r in range(CHUNKS)
    ]
    for load in loads:
        load.start()

    others = [(dy, dk) for dy in range(4) for dk in range(2) if (dy, dk) != (0, 0)]
    barrier = pltpu.get_barrier_semaphore()
    greeted = [right, left, beside, sibling, diagonal] + [peer(dy, dk) for dy, dk in others]
    for device in greeted:
        pl.semaphore_signal(barrier, inc=1, device_id=device, device_id_type=MESH)

    p = place
    query_count = counts[pairs[p, 0]]
    key_count = counts[pairs[p, 1]]
    row_top[...] = jnp.full(row_top.shape, NEGATIVE, jnp.float32)
    row_sum[...] = jnp.zeros(row_sum.shape, jnp.float32)
    col_top[...] = jnp.full(col_top.shape, NEGATIVE, jnp.float32)
    col_sum[...] = jnp.zeros(col_sum.shape, jnp.float32)
    for r in range(CHUNKS):
        lane = lax.broadcasted_iota(jnp.int32, (1, 128), 1)
        for m in range(MEMBERS):
            index = slot_index(half * 2 + m // 2, m % 2, r, lane)
            key_bias[r, :, pl.ds(m * 128, 128)] = jnp.where(index < key_count, 0.0, NEGATIVE)
        sub = lax.broadcasted_iota(jnp.int32, (128, 128), 0)
        query_bias[r] = jnp.where(slot_index(z, c, r, sub) < query_count, 0.0, NEGATIVE)

    pl.semaphore_wait(barrier, len(greeted))

    def remote(src, dst, send, recv, device):
        return pltpu.make_async_remote_copy(
            src_ref=src, dst_ref=dst, send_sem=send, recv_sem=recv,
            device_id=device, device_id_type=MESH,
        )

    started = []

    def go(copy):
        copy.start()
        started.append(copy)

    def own(r):
        return gathered[r].at[pl.ds(0, IMAGES)]

    from_left = lambda r: gathered[r].at[pl.ds(16, 16)]
    from_right = lambda r: gathered[r].at[pl.ds(48, 16)]
    far_low = lambda r: gathered[r].at[pl.ds(32, 8)]
    far_high = lambda r: gathered[r].at[pl.ds(40, 8)]

    def x_first(r):
        loads[r].wait()
        go(remote(own(r), from_left(r), xs.at[0, r], xr.at[0, r], right))
        go(remote(own(r), from_right(r), xs.at[1, r], xr.at[1, r], left))

    def landed(ref, send, recv):
        remote(ref, ref, send, recv, right).wait_recv()

    def x_second(r):
        landed(from_left(r), xs.at[0, r], xr.at[0, r])
        go(remote(gathered[r].at[pl.ds(16, 8)], far_low(r), xs.at[2, r], xr.at[2, r], right))
        landed(from_right(r), xs.at[1, r], xr.at[1, r])
        go(remote(gathered[r].at[pl.ds(56, 8)], far_high(r), xs.at[3, r], xr.at[3, r], left))

    def select(r):
        landed(far_low(r), xs.at[2, r], xr.at[2, r])
        landed(far_high(r), xs.at[3, r], xr.at[3, r])
        for pair in range(8):
            for side in range(2):
                image = pairs[pair, side]
                turn = lax.rem(x + 4 - image // IMAGES, 4)
                staged[r][pair, side] = gathered[r][turn * IMAGES + image % IMAGES]

    def spread(r):
        for dy in range(4):
            for dk in range(2):
                to = peer_place(dy, dk)
                e = dy * 2 + dk
                z_to = z if dk == 0 else 3 - z
                m_to = (z_to % 2) * 2 + c
                q_src, k_src = staged[r].at[to, 0], staged[r].at[to, 1]
                q_dst, k_dst = queries.at[r, place], keys.at[r, m_to, place]
                if e == 0:
                    for copy in (
                        pltpu.make_async_copy(q_src, q_dst, qr.at[r, place]),
                        pltpu.make_async_copy(k_src, k_dst, kr.at[r, place]),
                    ):
                        copy.start()
                else:
                    go(remote(k_src, k_dst, ks.at[r, e], kr.at[r, place], peer(dy, dk)))
                    go(remote(q_src, q_dst, qs.at[r, e], qr.at[r, place], peer(dy, dk)))

    def pass_keys(r):
        for s in range(SOURCES):
            landed(keys.at[r, member, s], ks.at[r, 0], kr.at[r, s])
        block = keys.at[r, member]
        go(remote(block, block, fs.at[0, r], fr.at[0, r], beside))
        go(remote(block, block, fs.at[1, r], fr.at[1, r], sibling))

    def pass_again(r):
        block = keys.at[r, member_beside]
        landed(block, fs.at[0, r], fr.at[0, r])
        go(remote(block, block, fs.at[2, r], fr.at[2, r], sibling))

    def tile(qi, kj):
        q = queries[qi].reshape(128, 256)
        k = keys[kj].reshape(512, 256)
        s = lax.dot_general(q, k, (((1,), (1,)), ((), ())), preferred_element_type=jnp.float32)
        kb = key_bias[kj]
        top = col_top[kj]
        tops = []
        high = top
        for g in range(8):
            rows = pl.ds(g * 16, 16)
            t = s[g * 16 : (g + 1) * 16] * scale + kb
            qb = query_bias[qi, rows, :]
            parts = [t[:, i * 128 : (i + 1) * 128] + qb for i in range(4)]
            for i in range(4):
                scores[qi, kj, rows, pl.ds(i * 128, 128)] = parts[i]
            tops.append(
                jnp.maximum(jnp.maximum(parts[0], parts[1]), jnp.maximum(parts[2], parts[3]))
            )
            both = jnp.concatenate(parts, axis=1)
            high = jnp.maximum(high, jnp.maximum(both[:8], both[8:]))
        total = col_sum[kj] * jnp.exp2(top - high)
        for g in range(8):
            rows = pl.ds(g * 16, 16)
            t = scores[qi, kj, rows, :]
            before = row_top[qi, rows, :]
            now = jnp.maximum(before, tops[g])
            acc = row_sum[qi, rows, :] * jnp.exp2(before - now)
            for i in range(4):
                acc += jnp.exp2(t[:, i * 128 : (i + 1) * 128] - now)
            row_sum[qi, rows, :] = acc
            row_top[qi, rows, :] = now
            total += jnp.exp2(t[:8] - high) + jnp.exp2(t[8:] - high)
        col_sum[kj] = total
        col_top[kj] = high

    def first_pass(r):
        for s in range(SOURCES):
            landed(queries.at[r, s], qs.at[r, 0], qr.at[r, s])
        landed(keys.at[r, parity * 2 + 1 - c], fs.at[1, r], fr.at[1, r])
        landed(keys.at[r, (1 - parity) * 2 + 1 - c], fs.at[2, r], fr.at[2, r])

        def body(n, carry):
            tile(jnp.minimum(n, r), jnp.where(n <= r, r, n - r - 1))
            return carry

        lax.fori_loop(0, 2 * r + 1, body, 0)

    x_first(0)
    x_first(1)
    for i in range(CHUNKS + 4):
        if i < CHUNKS:
            x_second(i)
            if i + 2 < CHUNKS:
                x_first(i + 2)
        if 0 <= i - 1 < CHUNKS:
            select(i - 1)
            spread(i - 1)
        if 0 <= i - 2 < CHUNKS:
            pass_keys(i - 2)
        if 0 <= i - 3 < CHUNKS:
            pass_again(i - 3)
        if 0 <= i - 4 < CHUNKS:
            first_pass(i - 4)

    for kj in range(CHUNKS):
        top = jnp.max(col_top[kj], axis=0, keepdims=True)
        total = jnp.sum(col_sum[kj] * jnp.exp2(col_top[kj] - top), axis=0, keepdims=True)
        for m in range(MEMBERS):
            stats[m, 0, pl.ds(kj, 1), :] = top[:, m * 128 : (m + 1) * 128]
            stats[m, 1, pl.ds(kj, 1), :] = total[:, m * 128 : (m + 1) * 128]
    team = [(1, sibling), (2, beside), (3, diagonal)]

    def mate(e):
        dh, dc = e // 2, e % 2
        return (1 - parity if dh else parity) * 2 + (1 - c if dc else c)

    for e, device in team:
        go(remote(stats.at[mate(e)], stats_got.at[member], cs.at[e], cr.at[e], device))

    lane = lax.broadcasted_iota(jnp.int32, (128, 128), 1)
    row_cols = jnp.zeros((128, 128), jnp.float32)
    for qi in range(CHUNKS):
        top = jnp.max(row_top[qi], axis=1, keepdims=True)
        total = jnp.sum(row_sum[qi] * jnp.exp2(row_top[qi] - top), axis=1, keepdims=True)
        row_cols = jnp.where(lane == qi, top + jnp.log2(total), row_cols)
    row_log = jnp.transpose(row_cols)[:8]

    for e, _ in team:
        landed(stats_got.at[mate(e)], cs.at[e], cr.at[e])
    tops = [stats[member, 0]] + [stats_got[mate(e), 0] for e, _ in team]
    sums = [stats[member, 1]] + [stats_got[mate(e), 1] for e, _ in team]
    highest = functools.reduce(jnp.maximum, tops)
    total = sum(b * jnp.exp2(a - highest) for a, b in zip(tops, sums))
    own_col = highest + jnp.log2(total)
    col_full[member] = own_col
    for e, device in team:
        go(remote(col_full.at[member], col_full.at[member], vs.at[e], vr.at[e], device))
    for e, _ in team:
        landed(col_full.at[mate(e)], vs.at[e], vr.at[e])

    def second(qi, carry):
        best = [None] * 8
        for kj in range(CHUNKS):
            halves = [col_full[m, pl.ds(kj, 1), :] * 0.5 for m in range(MEMBERS)]
            for g in range(8):
                t = scores[qi, kj, pl.ds(g * 16, 16), :]
                parts = [t[:, m * 128 : (m + 1) * 128] - halves[m] for m in range(MEMBERS)]
                part = jnp.maximum(
                    jnp.maximum(parts[0], parts[1]), jnp.maximum(parts[2], parts[3])
                )
                best[g] = part if kj == 0 else jnp.maximum(best[g], part)
        for g in range(8):
            rows = pl.ds(g * 16, 16)
            most = jnp.max(best[g], axis=1, keepdims=True)
            best_cols[rows, :] = jnp.where(lane[:16] == qi, most, best_cols[rows, :])
        return carry

    best_cols[...] = jnp.zeros((128, 128), jnp.float32)
    lax.fori_loop(0, CHUNKS, second, 0)
    best = 2.0 * jnp.transpose(best_cols[...])[:8] - row_log

    chunk = lax.broadcasted_iota(jnp.int32, (8, 128), 0)
    lane8 = lax.broadcasted_iota(jnp.int32, (8, 128), 1)
    index = slot_index(z, c, chunk, lane8)
    query_valid = index < query_count
    results = (
        jnp.where(query_valid, row_log * LN2, 0.0),
        jnp.where(index < key_count, own_col * LN2, 0.0),
        jnp.where(query_valid, best * LN2, 0.0),
    )
    for j, value in enumerate(results):
        value = block_transpose(value)
        for s in range(SOURCES):
            sent[s, pl.ds(j, 1), :] = value[s : s + 1]
    for dy in range(4):
        for dk in range(2):
            e = dy * 2 + dk
            to = peer_place(dy, dk)
            if e == 0:
                pltpu.make_async_copy(sent.at[to], got.at[place], or_.at[place]).start()
            else:
                go(remote(sent.at[to], got.at[place], os_.at[e], or_.at[place], peer(dy, dk)))
    for s in range(SOURCES):
        landed(got.at[s], os_.at[0], or_.at[s])
    for s in range(SOURCES):
        out_row[pl.ds(s, 1), :] = got[s, pl.ds(0, 1), :]
        out_col[pl.ds(s, 1), :] = got[s, pl.ds(1, 1), :]
        out_best[pl.ds(s, 1), :] = got[s, pl.ds(2, 1), :]
    for copy in started:
        copy.wait_send()


def local(descriptors, pairs, counts):
    scale = 2.0 / math.sqrt(descriptors.shape[2]) * LOG2E
    width = descriptors.shape[2]
    bf16, f32 = jnp.bfloat16, jnp.float32
    dma = pltpu.SemaphoreType.DMA
    scratch = [pltpu.VMEM((GROUPS * IMAGES, ROWS, width), bf16) for _ in range(CHUNKS)]
    scratch += [pltpu.VMEM((8, 2, ROWS, width), bf16) for _ in range(CHUNKS)]
    scratch += [
        pltpu.VMEM((CHUNKS, SOURCES, ROWS, width), bf16),
        pltpu.VMEM((CHUNKS, MEMBERS, SOURCES, ROWS, width), bf16),
        pltpu.VMEM((CHUNKS, CHUNKS, 128, 512), f32),
        pltpu.VMEM((CHUNKS, 128, 128), f32),
        pltpu.VMEM((CHUNKS, 128, 128), f32),
        pltpu.VMEM((CHUNKS, 8, 512), f32),
        pltpu.VMEM((CHUNKS, 8, 512), f32),
        pltpu.VMEM((CHUNKS, 1, 512), f32),
        pltpu.VMEM((CHUNKS, 128, 128), f32),
        pltpu.VMEM((MEMBERS, 2, 8, 128), f32),
        pltpu.VMEM((MEMBERS, 2, 8, 128), f32),
        pltpu.VMEM((MEMBERS, 8, 128), f32),
        pltpu.VMEM((128, 128), f32),
        pltpu.VMEM((8, 8, 128), f32),
        pltpu.VMEM((8, 8, 128), f32),
        dma((CHUNKS,)),
        dma((4, CHUNKS)), dma((4, CHUNKS)),
        dma((CHUNKS, 8)), dma((CHUNKS, 8)),
        dma((CHUNKS, 8)), dma((CHUNKS, 8)),
        dma((3, CHUNKS)), dma((3, CHUNKS)),
        dma((4,)), dma((4,)),
        dma((4,)), dma((4,)),
        dma((8,)), dma((8,)),
    ]
    out = jax.ShapeDtypeStruct((8, 128), f32)
    return pl.pallas_call(
        functools.partial(kernel, scale),
        out_shape=(out, out, out),
        in_specs=[
            pl.BlockSpec(memory_space=pltpu.SMEM),
            pl.BlockSpec(memory_space=pltpu.SMEM),
            pl.BlockSpec(memory_space=pl.ANY),
        ],
        out_specs=[pl.BlockSpec(memory_space=pltpu.VMEM)] * 3,
        scratch_shapes=scratch,
        compiler_params=pltpu.CompilerParams(
            collective_id=0, has_side_effects=True, vmem_limit_bytes=48 * 1024 * 1024
        ),
    )(pairs, counts, descriptors)


def solution(mesh):
    torus = Mesh(
        mesh.devices.reshape(mesh.shape["grp"], 4, 4, 2), ("grp", "tile_0", "tile_1", "tile_2")
    )
    return jax.shard_map(
        local,
        mesh=torus,
        in_specs=(P("grp", TILE, None), P("grp", None), P()),
        out_specs=(P("grp", TILE), P("grp", TILE), P("grp", TILE)),
        check_vma=False,
    )
```

time: 199 us -> 84.9 us (0.43)
  waiting for transfers between devices: 103 us -> 0 us
  Pallas kernels: 0 us -> 80.4 us
  starting transfers between devices: 20.5 us -> 0 us
  other arithmetic: 20.3 us -> 0 us
  blocking collectives: 14.8 us -> 0 us
  matrix products: 13.9 us -> 0 us
  between operations: 14.3 us -> 0.65 us
  local copies, waits for them, and re-layouts: 11.7 us -> 3.77 us
    pallas_call x0 -> x1, Pallas kernels: none -> 80.4 us  [local(): pl.pallas_call(functools.partial(kernel, scale), out_shape=(out, out, out...]
    all_gather x1 -> x0, waiting for transfers between devices: 52.2 us -> none  [local(): image_rows = lax.all_gather(descriptors, 'grp', axis=0, tiled=True)]
    all_to_all x4 -> x0, waiting for transfers between devices: 50.1 us -> none  [the longest x1 32.2 us: in_one_piece(): lax.all_to_all(both, axis, split_axis=split_dim, concat_axis=concat_dim,...]
    all_to_all x4 -> x0, starting transfers between devices: 20.4 us -> none  [the longest x1 7.87 us: in_one_piece(): lax.all_to_all(both, axis, split_axis=split_dim, concat_axis=concat_dim,...]
    all_to_all x2 -> x0, blocking collectives: 14.8 us -> none  [the longest x1 11.1 us: in_one_piece(): lax.all_to_all(both, axis, split_axis=split_dim, concat_axis=concat_dim,...]
    dot_general x4 -> x0, matrix products: 13.9 us -> none  [the longest x2 7.9 us: first_pass(): jnp.einsum('qd,kd->qk', block_rows, key_image, preferred_element_type=jnp...]
    reduce_sum x3 -> x0, other arithmetic: 9.91 us -> none  [the longest x2 9.7 us: first_pass(): jnp.sum(jnp.where(key_mask, jnp.exp(scores - row_top[:, None]), 0.0), axi...]
    gather x2 -> x0, local copies, waits for them, and re-layouts: 5.54 us -> none  [the longest x1 2.78 us: local(): keys_local = jnp.take(image_rows, second, axis=0)]
  transfers between devices with their start and end apart: 5 -> 0, of which waited for: 5 -> 0; matrix products, arithmetic and copies ran while one was open for 3% -> 0% of each run, Pallas kernels for 0% -> 0%
where the time goes in v1:
time: 84.9 us; the launch traced here: 84.8 us
  Pallas kernels  80.4 us (95%)
  local copies, waits for them, and re-layouts  3.77 us (4%)
    pallas_call x1, Pallas kernels, local(): pl.pallas_call(functools.partial(kernel, scale), out_shape=(out, out, out...  80.4 us
    unnamed x8, local copies, waits for them, and re-layouts  3.77 us

profile of v1, /device:TPU:1, one launch (start us, length us, event | category | flops | bytes accessed | tf_op | source)
XLA Modules:
  0.0 84.8 jit_solution(18074380643756518968)
XLA Ops:
  0.6 0.0 copy-start.1
  0.6 0.8 copy.6.pairs
  1.4 0.0 copy-done.1
  1.4 0.0 copy-start
  1.4 1.2 %copy-done = bf16[16,128,256]{2,1,0:T(8,128)(2,1)S(1)} copy-done((bf16[16,128,256]{2,1,0:T(8,128)(2,1)S(1)}, bf16[16,128,256]{2,1,0:T(8,128)(2,1)}, u32[]{:S(2)}) %copy-start) | copy-done | bytes 1048600
  2.6 80.4 %shard_map.58 = (f32[8,128]{1,0:T(8,128)S(1)}, f32[8,128]{1,0:T(8,128)S(1)}, f32[8,128]{1,0:T(8,128)S(1)}) custom-call(s32[8,2]{1,0:T(8,128)S(1)} %copy.6.pairs, s32[64]{0:T(128)S(1)} %copy-done.1, bf16[16,128,256]{2,1,0:T(8,128)(2,1)S(1)} %copy-done), custom_call_target="tpu_custom_call" | custom-call | tf_op jit(solution)/shard_map/pallas_call | solution.py:364
  83.0 0.6 copy.10
  83.6 0.6 copy.11
  84.2 0.6 copy.12
Async XLA Ops:
  0.6 0.8 copy-start.1
  1.4 1.2 %copy-start = (bf16[16,128,256]{2,1,0:T(8,128)(2,1)S(1)}, bf16[16,128,256]{2,1,0:T(8,128)(2,1)}, u32[]{:S(2)}) copy-start(bf16[16,128,256]{2,1,0:T(8,128)(2,1)} %desc.1) | copy-start | bytes 3145732

commit v2 on v1

--- a/solution.py
+++ b/solution.py
@@ -43,13 +43,13 @@
     return out
 
 
-def kernel(scale, pairs, counts, desc, out_row, out_col, out_best, *scratch):
+def kernel(scale, pairs, counts, desc, out, *scratch):
     gathered = scratch[:CHUNKS]
     staged = scratch[CHUNKS : 2 * CHUNKS]
     (
         queries, keys, scores, row_top, row_sum, col_top, col_sum, key_bias, query_bias,
-        stats, stats_got, col_full, best_cols, sent, got,
-        load_sem, xs, xr, qs, qr, ks, kr, fs, fr, cs, cr, vs, vr, os_, or_,
+        col_log, col_half, best_cols, held_even, held_odd, sent, got,
+        load_sem, xs, xr, qs, qr, ks, kr, fs, fr, cs, cr, os_, or_,
     ) = scratch[2 * CHUNKS :]
     x, y, z, c = (lax.axis_index(a) for a in ("grp",) + TILE)
     right = (lax.rem(x + 1, 4), y, z, c)
@@ -86,8 +86,8 @@
         pl.semaphore_signal(barrier, inc=1, device_id=device, device_id_type=MESH)
 
     p = place
-    query_count = counts[pairs[p, 0]]
-    key_count = counts[pairs[p, 1]]
+    query_count = counts[pairs[0, p]]
+    key_count = counts[pairs[1, p]]
     row_top[...] = jnp.full(row_top.shape, NEGATIVE, jnp.float32)
     row_sum[...] = jnp.zeros(row_sum.shape, jnp.float32)
     col_top[...] = jnp.full(col_top.shape, NEGATIVE, jnp.float32)
@@ -141,7 +141,7 @@
         landed(far_high(r), xs.at[3, r], xr.at[3, r])
         for pair in range(8):
             for side in range(2):
-                image = pairs[pair, side]
+                image = pairs[side, pair]
                 turn = lax.rem(x + 4 - image // IMAGES, 4)
                 staged[r][pair, side] = gathered[r][turn * IMAGES + image % IMAGES]
 
@@ -176,30 +176,34 @@
         landed(block, fs.at[0, r], fr.at[0, r])
         go(remote(block, block, fs.at[2, r], fr.at[2, r], sibling))
 
-    def tile(qi, kj):
+    def product(qi, kj, held):
         q = queries[qi].reshape(128, 256)
         k = keys[kj].reshape(512, 256)
-        s = lax.dot_general(q, k, (((1,), (1,)), ((), ())), preferred_element_type=jnp.float32)
+        held[...] = lax.dot_general(
+            q, k, (((1,), (1,)), ((), ())), preferred_element_type=jnp.float32
+        )
+
+    def fold(qi, kj, held):
         kb = key_bias[kj]
         top = col_top[kj]
         tops = []
         high = top
         for g in range(8):
             rows = pl.ds(g * 16, 16)
-            t = s[g * 16 : (g + 1) * 16] * scale + kb
+            t = held[rows, :] * scale + kb
             qb = query_bias[qi, rows, :]
             parts = [t[:, i * 128 : (i + 1) * 128] + qb for i in range(4)]
-            for i in range(4):
-                scores[qi, kj, rows, pl.ds(i * 128, 128)] = parts[i]
             tops.append(
                 jnp.maximum(jnp.maximum(parts[0], parts[1]), jnp.maximum(parts[2], parts[3]))
             )
             both = jnp.concatenate(parts, axis=1)
+            scores[qi, kj, rows, :] = both
+            held[rows, :] = both
             high = jnp.maximum(high, jnp.maximum(both[:8], both[8:]))
         total = col_sum[kj] * jnp.exp2(top - high)
         for g in range(8):
             rows = pl.ds(g * 16, 16)
-            t = scores[qi, kj, rows, :]
+            t = held[rows, :]
             before = row_top[qi, rows, :]
             now = jnp.maximum(before, tops[g])
             acc = row_sum[qi, rows, :] * jnp.exp2(before - now)
@@ -217,11 +221,19 @@
         landed(keys.at[r, parity * 2 + 1 - c], fs.at[1, r], fr.at[1, r])
         landed(keys.at[r, (1 - parity) * 2 + 1 - c], fs.at[2, r], fr.at[2, r])
 
+        def at(n):
+            return jnp.minimum(n, r), jnp.where(n <= r, r, n - r - 1)
+
         def body(n, carry):
-            tile(jnp.minimum(n, r), jnp.where(n <= r, r, n - r - 1))
+            product(*at(2 * n + 1), held_odd)
+            fold(*at(2 * n), held_even)
+            product(*at(2 * n + 2), held_even)
+            fold(*at(2 * n + 1), held_odd)
             return carry
 
-        lax.fori_loop(0, 2 * r + 1, body, 0)
+        product(*at(0), held_even)
+        lax.fori_loop(0, r, body, 0)
+        fold(*at(2 * r), held_even)
 
     x_first(0)
     x_first(1)
@@ -243,9 +255,7 @@
     for kj in range(CHUNKS):
         top = jnp.max(col_top[kj], axis=0, keepdims=True)
         total = jnp.sum(col_sum[kj] * jnp.exp2(col_top[kj] - top), axis=0, keepdims=True)
-        for m in range(MEMBERS):
-            stats[m, 0, pl.ds(kj, 1), :] = top[:, m * 128 : (m + 1) * 128]
-            stats[m, 1, pl.ds(kj, 1), :] = total[:, m * 128 : (m + 1) * 128]
+        col_log[member, kj] = top + jnp.log2(total)
     team = [(1, sibling), (2, beside), (3, diagonal)]
 
     def mate(e):
@@ -253,7 +263,7 @@
         return (1 - parity if dh else parity) * 2 + (1 - c if dc else c)
 
     for e, device in team:
-        go(remote(stats.at[mate(e)], stats_got.at[member], cs.at[e], cr.at[e], device))
+        go(remote(col_log.at[member], col_log.at[member], cs.at[e], cr.at[e], device))
 
     lane = lax.broadcasted_iota(jnp.int32, (128, 128), 1)
     row_cols = jnp.zeros((128, 128), jnp.float32)
@@ -264,25 +274,28 @@
     row_log = jnp.transpose(row_cols)[:8]
 
     for e, _ in team:
-        landed(stats_got.at[mate(e)], cs.at[e], cr.at[e])
-    tops = [stats[member, 0]] + [stats_got[mate(e), 0] for e, _ in team]
-    sums = [stats[member, 1]] + [stats_got[mate(e), 1] for e, _ in team]
-    highest = functools.reduce(jnp.maximum, tops)
-    total = sum(b * jnp.exp2(a - highest) for a, b in zip(tops, sums))
-    own_col = highest + jnp.log2(total)
-    col_full[member] = own_col
-    for e, device in team:
-        go(remote(col_full.at[member], col_full.at[member], vs.at[e], vr.at[e], device))
-    for e, _ in team:
-        landed(col_full.at[mate(e)], vs.at[e], vr.at[e])
+        landed(col_log.at[mate(e)], cs.at[e], cr.at[e])
+    cols = []
+    for kj in range(CHUNKS):
+        logs = [col_log[m, kj] for m in range(MEMBERS)]
+        top = jnp.maximum(jnp.maximum(logs[0], logs[1]), jnp.maximum(logs[2], logs[3]))
+        total = sum(jnp.exp2(v - top) for v in logs)
+        full = top + jnp.log2(total)
+        col_half[kj] = full * 0.5
+        mine = full[:, :128]
+        for m in range(1, MEMBERS):
+            mine = jnp.where(member == m, full[:, m * 128 : (m + 1) * 128], mine)
+        cols.append(mine)
+    own_col = jnp.concatenate(cols, axis=0)
 
     def second(qi, carry):
         best = [None] * 8
         for kj in range(CHUNKS):
-            halves = [col_full[m, pl.ds(kj, 1), :] * 0.5 for m in range(MEMBERS)]
+            half_log = col_half[kj]
             for g in range(8):
                 t = scores[qi, kj, pl.ds(g * 16, 16), :]
-                parts = [t[:, m * 128 : (m + 1) * 128] - halves[m] for m in range(MEMBERS)]
+                t = t - half_log
+                parts = [t[:, m * 128 : (m + 1) * 128] for m in range(MEMBERS)]
                 part = jnp.maximum(
                     jnp.maximum(parts[0], parts[1]), jnp.maximum(parts[2], parts[3])
                 )
@@ -321,9 +334,8 @@
     for s in range(SOURCES):
         landed(got.at[s], os_.at[0], or_.at[s])
     for s in range(SOURCES):
-        out_row[pl.ds(s, 1), :] = got[s, pl.ds(0, 1), :]
-        out_col[pl.ds(s, 1), :] = got[s, pl.ds(1, 1), :]
-        out_best[pl.ds(s, 1), :] = got[s, pl.ds(2, 1), :]
+        for j in range(3):
+            out[j, pl.ds(s, 1), :] = got[s, pl.ds(j, 1), :]
     for copy in started:
         copy.wait_send()
 
@@ -345,10 +357,11 @@
         pltpu.VMEM((CHUNKS, 8, 512), f32),
         pltpu.VMEM((CHUNKS, 1, 512), f32),
         pltpu.VMEM((CHUNKS, 128, 128), f32),
-        pltpu.VMEM((MEMBERS, 2, 8, 128), f32),
-        pltpu.VMEM((MEMBERS, 2, 8, 128), f32),
-        pltpu.VMEM((MEMBERS, 8, 128), f32),
+        pltpu.VMEM((MEMBERS, CHUNKS, 1, 512), f32),
+        pltpu.VMEM((CHUNKS, 1, 512), f32),
         pltpu.VMEM((128, 128), f32),
+        pltpu.VMEM((128, 512), f32),
+        pltpu.VMEM((128, 512), f32),
         pltpu.VMEM((8, 8, 128), f32),
         pltpu.VMEM((8, 8, 128), f32),
         dma((CHUNKS,)),
@@ -357,24 +370,23 @@
         dma((CHUNKS, 8)), dma((CHUNKS, 8)),
         dma((3, CHUNKS)), dma((3, CHUNKS)),
         dma((4,)), dma((4,)),
-        dma((4,)), dma((4,)),
         dma((8,)), dma((8,)),
     ]
-    out = jax.ShapeDtypeStruct((8, 128), f32)
-    return pl.pallas_call(
+    out = pl.pallas_call(
         functools.partial(kernel, scale),
-        out_shape=(out, out, out),
+        out_shape=jax.ShapeDtypeStruct((3, 8, 128), f32),
         in_specs=[
             pl.BlockSpec(memory_space=pltpu.SMEM),
             pl.BlockSpec(memory_space=pltpu.SMEM),
             pl.BlockSpec(memory_space=pl.ANY),
         ],
-        out_specs=[pl.BlockSpec(memory_space=pltpu.VMEM)] * 3,
+        out_specs=pl.BlockSpec(memory_space=pltpu.VMEM),
         scratch_shapes=scratch,
         compiler_params=pltpu.CompilerParams(
-            collective_id=0, has_side_effects=True, vmem_limit_bytes=48 * 1024 * 1024
+            collective_id=0, has_side_effects=True, vmem_limit_bytes=63 * 1024 * 1024
         ),
-    )(pairs, counts, descriptors)
+    )(pairs.T, counts, descriptors)
+    return out[0], out[1], out[2]
 
 
 def solution(mesh):

time: 84.9 us -> 76.6 us (0.902)
  Pallas kernels: 80.4 us -> 74.5 us
  local copies, waits for them, and re-layouts: 3.77 us -> 1.29 us
    pallas_call x1, Pallas kernels: 80.4 us -> 74.5 us  [local(): pl.pallas_call(functools.partial(kernel, scale), out_shape=jax.ShapeDtype...]
    unnamed x8 -> x0, local copies, waits for them, and re-layouts: 3.77 us -> none
    squeeze x0 -> x1, local copies, waits for them, and re-layouts: none -> 1.29 us  [local(): return (out[0], out[1], out[2])]
where the time goes in v2:
time: 76.6 us; the launch traced here: 76.4 us
  Pallas kernels  74.5 us (97%)
  local copies, waits for them, and re-layouts  1.29 us (2%)
    pallas_call x1, Pallas kernels, local(): pl.pallas_call(functools.partial(kernel, scale), out_shape=jax.ShapeDtype...  74.5 us

profile of v2, /device:TPU:1, one launch (start us, length us, event | category | flops | bytes accessed | tf_op | source)
XLA Modules:
  0.0 76.4 jit_solution(16240740312094465594)
XLA Ops:
  0.6 74.5 %shard_map.58 = f32[3,8,128]{2,1,0:T(8,128)} custom-call(s32[2,8]{1,0:T(2,128)} %bitcast.7, s32[64]{0:T(128)} %counts.1, bf16[16,128,256]{2,1,0:T(8,128)(2,1)} %desc.1), custom_call_target="tpu_custom_call" | custom-call | tf_op jit(solution)/shard_map/pallas_call | solution.py:375
  75.1 1.3 %slice_bitcast_fusion = (f32[8,128]{1,0:T(8,128)}, f32[8,128]{1,0:T(8,128)}, f32[8,128]{1,0:T(8,128)}) fusion(f32[3,8,128]{2,1,0:T(8,128)} %shard_map.58), kind=kLoop, calls=%fused_computation | loop fusion | bytes 24576 | tf_op jit(solution)/shard_map/squeeze | solution.py:389

commit v3 on v2

--- a/solution.py
+++ b/solution.py
@@ -19,6 +19,9 @@
 IMAGES = 16
 SOURCES = 8
 MEMBERS = 4
+ENTER = 10
+RELAY = 5
+WIDE = 1
 LOG2E = math.log2(math.e)
 LN2 = math.log(2.0)
 
@@ -43,7 +46,59 @@
     return out
 
 
-def kernel(scale, pairs, counts, desc, out, *scratch):
+def route(pairs, group, x):
+    slots = []
+    for pair in range(8):
+        for side in range(2):
+            image = pairs[group, side, pair]
+            slots.append((lax.rem(image // IMAGES - group + GROUPS, GROUPS), lax.rem(image, IMAGES)))
+    one = [[jnp.where(d == k, 1, 0) for d, _ in slots] for k in range(GROUPS)]
+    near, far, behind = (sum(one[k]) for k in (1, 2, 3))
+    least = jnp.maximum(jnp.maximum(far - RELAY, behind + far - ENTER), 0)
+    most = jnp.minimum(jnp.minimum(far, RELAY), ENTER - near)
+    by_right = jnp.minimum(jnp.maximum((behind + far - near + 1) // 2, least), most)
+    rank = [0] * GROUPS
+    routed = []
+    for s, (d, image) in enumerate(slots):
+        relay_left = rank[2] - by_right
+        by_left = jnp.logical_or(d == 3, jnp.logical_and(d == 2, relay_left >= 0))
+        from_right = jnp.logical_or(d == 1, jnp.logical_and(d == 2, relay_left < 0))
+        right_place = jnp.where(d == 1, rank[1], near + rank[2])
+        left_place = jnp.where(d == 3, rank[3], behind + relay_left)
+        routed.append(
+            (
+                d, image,
+                jnp.where(from_right, right_place, -1), jnp.where(by_left, left_place, -1),
+                jnp.where(jnp.logical_and(d == 2, relay_left < 0), rank[2], -1),
+                jnp.where(jnp.logical_and(d == 2, relay_left >= 0), relay_left, -1),
+            )
+        )
+        for k in range(1, GROUPS):
+            rank[k] = rank[k] + one[k][s]
+    return routed, jnp.where(least > most, 1, 0)
+
+
+def at_place(entries, k):
+    return sum(jnp.where(place == k, value, 0) for place, value in entries)
+
+
+def within(value, count):
+    return jnp.minimum(jnp.maximum(value, 0), count - 1)
+
+
+def kernel(scale, narrow, pairs, counts, desc, out, *scratch):
+    if narrow:
+        misfit, scratch = scratch[0], scratch[1:]
+        every_pair, relay_code, enter_code, slot_code = scratch[-4:]
+        middle, arrived, packed_middle, packed_arrived = (
+            scratch[-4 - (4 - k) * CHUNKS : -4 - (3 - k) * CHUNKS] for k in range(4)
+        )
+        ps, pr = scratch[-4 - 4 * CHUNKS - 2 : -4 - 4 * CHUNKS]
+        scratch = scratch[: -4 - 4 * CHUNKS - 2]
+
+    def wide(r):
+        return not narrow or r < WIDE
+
     gathered = scratch[:CHUNKS]
     staged = scratch[CHUNKS : 2 * CHUNKS]
     (
@@ -61,6 +116,7 @@
     z_beside = half * 2 + (1 - parity)
     beside = (x, y, z_beside, c)
     sibling = (x, y, z, 1 - c)
+    opposite = (lax.rem(x + 2, 4), y, z, c)
     diagonal = (x, y, z_beside, 1 - c)
     member_beside = (1 - parity) * 2 + c
 
@@ -82,6 +138,8 @@
     others = [(dy, dk) for dy in range(4) for dk in range(2) if (dy, dk) != (0, 0)]
     barrier = pltpu.get_barrier_semaphore()
     greeted = [right, left, beside, sibling, diagonal] + [peer(dy, dk) for dy, dk in others]
+    if narrow:
+        greeted.append(opposite)
     for device in greeted:
         pl.semaphore_signal(barrier, inc=1, device_id=device, device_id_type=MESH)
 
@@ -124,19 +182,53 @@
 
     def x_first(r):
         loads[r].wait()
+        if not wide(r):
+            for k in range(2 * RELAY):
+                packed_middle[r][k] = gathered[r][relay_code[k]]
+            for k, device in ((0, left), (1, right)):
+                part = pl.ds(k * RELAY, RELAY)
+                go(remote(
+                    packed_middle[r].at[part], middle[r].at[part], xs.at[k, r], xr.at[k, r], device
+                ))
+            return
         go(remote(own(r), from_left(r), xs.at[0, r], xr.at[0, r], right))
         go(remote(own(r), from_right(r), xs.at[1, r], xr.at[1, r], left))
 
     def landed(ref, send, recv):
         remote(ref, ref, send, recv, right).wait_recv()
 
+    def choose(code, first, other):
+        a = first[jnp.minimum(code, IMAGES - 1)]
+        b = other[jnp.maximum(code - IMAGES, 0)]
+        return lax.select(code < IMAGES, a, b)
+
     def x_second(r):
+        if not wide(r):
+            for k in range(2):
+                landed(middle[r].at[pl.ds(k * RELAY, RELAY)], xs.at[k, r], xr.at[k, r])
+            for k, device in ((0, left), (1, right)):
+                for n in range(k * ENTER, (k + 1) * ENTER):
+                    packed_arrived[r][n] = choose(enter_code[n], gathered[r], middle[r])
+                part = pl.ds(k * ENTER, ENTER)
+                go(remote(
+                    packed_arrived[r].at[part], arrived[r].at[part],
+                    xs.at[2 + k, r], xr.at[2 + k, r], device,
+                ))
+            return
         landed(from_left(r), xs.at[0, r], xr.at[0, r])
         go(remote(gathered[r].at[pl.ds(16, 8)], far_low(r), xs.at[2, r], xr.at[2, r], right))
         landed(from_right(r), xs.at[1, r], xr.at[1, r])
         go(remote(gathered[r].at[pl.ds(56, 8)], far_high(r), xs.at[3, r], xr.at[3, r], left))
 
     def select(r):
+        if not wide(r):
+            for k in range(2):
+                landed(arrived[r].at[pl.ds(k * ENTER, ENTER)], xs.at[2 + k, r], xr.at[2 + k, r])
+            for pair in range(8):
+                for side in range(2):
+                    code = slot_code[pair * 2 + side]
+                    staged[r][pair, side] = choose(code, gathered[r], arrived[r])
+            return
         landed(far_low(r), xs.at[2, r], xr.at[2, r])
         landed(far_high(r), xs.at[3, r], xr.at[3, r])
         for pair in range(8):
@@ -235,7 +327,48 @@
         lax.fori_loop(0, r, body, 0)
         fold(*at(2 * r), held_even)
 
+    def work_out_routes():
+        for side in range(2):
+            for pair in range(8):
+                every_pair[x, side, pair] = pairs[side, pair]
+        for e in range(1, GROUPS):
+            other = lax.rem(x + e, GROUPS)
+            landed(every_pair.at[other], ps.at[e], pr.at[e])
+        before, after, across = (lax.rem(x + k, GROUPS) for k in (3, 1, 2))
+        routed, bad = route(every_pair, x, x)
+        for s, (d, image, right_place, left_place, _, _) in enumerate(routed):
+            far = jnp.where(
+                right_place >= 0, within(right_place, ENTER), ENTER + within(left_place, ENTER)
+            )
+            slot_code[s] = jnp.where(d == 0, image, IMAGES + far)
+        routed, now = route(every_pair, before, x)
+        bad += now
+        entries = [
+            (p, jnp.where(d == 1, i, IMAGES + within(m, RELAY))) for d, i, p, _, m, _ in routed
+        ]
+        for k in range(ENTER):
+            enter_code[k] = at_place(entries, k)
+        routed, now = route(every_pair, after, x)
+        bad += now
+        entries = [
+            (p, jnp.where(d == 3, i, IMAGES + RELAY + within(m, RELAY)))
+            for d, i, _, p, _, m in routed
+        ]
+        for k in range(ENTER):
+            enter_code[ENTER + k] = at_place(entries, k)
+        routed, now = route(every_pair, across, x)
+        bad += now
+        for k in range(RELAY):
+            relay_code[k] = at_place([(m, i) for _, i, _, _, m, _ in routed], k)
+            relay_code[RELAY + k] = at_place([(m, i) for _, i, _, _, _, m in routed], k)
+        misfit[...] = jnp.full(misfit.shape, bad, jnp.int32)
+
+    if narrow:
+        for e, device in ((3, right), (1, left), (2, opposite)):
+            go(remote(pairs, every_pair.at[x], ps.at[e], pr.at[e], device))
     x_first(0)
+    if narrow:
+        work_out_routes()
     x_first(1)
     for i in range(CHUNKS + 4):
         if i < CHUNKS:
@@ -372,21 +505,46 @@
         dma((4,)), dma((4,)),
         dma((8,)), dma((8,)),
     ]
-    out = pl.pallas_call(
-        functools.partial(kernel, scale),
-        out_shape=jax.ShapeDtypeStruct((3, 8, 128), f32),
-        in_specs=[
-            pl.BlockSpec(memory_space=pltpu.SMEM),
-            pl.BlockSpec(memory_space=pltpu.SMEM),
-            pl.BlockSpec(memory_space=pl.ANY),
-        ],
-        out_specs=pl.BlockSpec(memory_space=pltpu.VMEM),
-        scratch_shapes=scratch,
-        compiler_params=pltpu.CompilerParams(
-            collective_id=0, has_side_effects=True, vmem_limit_bytes=63 * 1024 * 1024
-        ),
-    )(pairs.T, counts, descriptors)
-    return out[0], out[1], out[2]
+    smem, vmem = pltpu.SMEM, pltpu.VMEM
+
+    def call(narrow):
+        rooms = list(scratch)
+        if narrow:
+            rooms[WIDE:CHUNKS] = [vmem((IMAGES, ROWS, width), bf16)] * (CHUNKS - WIDE)
+            rooms += [dma((GROUPS,)), dma((GROUPS,))]
+            for room in (RELAY, ENTER, RELAY, ENTER):
+                rooms += [vmem((2 * room, ROWS, width), bf16)] * CHUNKS
+            rooms += [
+                smem((GROUPS, 2, 8), jnp.int32),
+                smem((2 * RELAY,), jnp.int32),
+                smem((2 * ENTER,), jnp.int32),
+                smem((IMAGES,), jnp.int32),
+            ]
+        shapes = [jax.ShapeDtypeStruct((3, 8, 128), f32), jax.ShapeDtypeStruct((8, 128), jnp.int32)]
+        count = 2 if narrow else 1
+        return pl.pallas_call(
+            functools.partial(kernel, scale, narrow),
+            out_shape=shapes[:count],
+            in_specs=[
+                pl.BlockSpec(memory_space=smem),
+                pl.BlockSpec(memory_space=smem),
+                pl.BlockSpec(memory_space=pl.ANY),
+            ],
+            out_specs=[pl.BlockSpec(memory_space=vmem)] * count,
+            scratch_shapes=rooms,
+            name="narrow" if narrow else "full",
+            compiler_params=pltpu.CompilerParams(
+                collective_id=1 if narrow else 0,
+                has_side_effects=True,
+                vmem_limit_bytes=63 * 1024 * 1024,
+            ),
+        )(pairs.T, counts, descriptors)
+
+    def split(out):
+        return out[0], out[1], out[2]
+
+    out, misfit = call(True)
+    return lax.cond(misfit[0, 0] > 0, lambda _: split(call(False)[0]), split, out)
 
 
 def solution(mesh):

time: 76.6 us -> 75.6 us (0.987)
  Pallas kernels: 74.5 us -> 71.4 us
  local copies, waits for them, and re-layouts: 1.29 us -> 2.47 us
    pallas_call x1, Pallas kernels: 74.5 us -> 71.4 us  [call(): pl.pallas_call(functools.partial(kernel, scale, narrow), out_shape=shapes...]
    slice x0 -> x1, local copies, waits for them, and re-layouts: none -> 1.2 us  [local(): misfit[0, 0] > 0]
where the time goes in v3:
time: 75.6 us; the launch traced here: 75.4 us
  Pallas kernels  71.4 us (94%)
  local copies, waits for them, and re-layouts  2.47 us (3%)
  between operations  1.32 us (2%)
    pallas_call x1, Pallas kernels, call(): pl.pallas_call(functools.partial(kernel, scale, narrow), out_shape=shapes...  71.4 us

profile of v3, /device:TPU:1, one launch (start us, length us, event | category | flops | bytes accessed | tf_op | source)
XLA Modules:
  0.0 75.4 jit_solution(2439986022289705526)
XLA Ops:
  0.6 0.0 copy-start
  0.6 0.0 copy-start.1
  0.7 0.7 copy-done
  1.3 0.0 copy-done.1
  1.3 71.4 %narrow.1 = (f32[3,8,128]{2,1,0:T(8,128)S(1)}, s32[8,128]{1,0:T(8,128)}) custom-call(s32[2,8]{1,0:T(2,128)S(1)} %bitcast.9, s32[64]{0:T(128)S(1)} %copy-done.1, bf16[16,128,256]{2,1,0:T(8,128)(2,1)} %desc.1), custom_call_target="tpu_custom_call" | custom-call | tf_op jit(solution)/shard_map/narrow/pallas_call | solution.py:525
  72.7 1.2 %slice.21 = s32[1,1]{1,0:T(1,128)} slice(s32[8,128]{1,0:T(8,128)} %get-tuple-element.15), slice={[0:1], [0:1]} | slice | bytes 8 | tf_op jit(solution)/shard_map/slice | solution.py:547
  74.6 0.2 conditional.1
  74.8 0.6 slice_bitcast_fusion.2
Async XLA Ops:
  0.6 0.7 copy-start
  0.6 0.7 copy-start.1

commit v4 on v3

--- a/solution.py
+++ b/solution.py
@@ -19,9 +19,20 @@
 IMAGES = 16
 SOURCES = 8
 MEMBERS = 4
-ENTER = 10
-RELAY = 5
+ENTER = 9
+RELAY = 4
 WIDE = 1
+ORDER = (
+    ("first", 1), ("second", 0), ("first", 2), ("first", 3), ("second", 1), ("first", 4),
+    ("spread", 0), ("second", 2), ("first", 5), ("second", 3), ("first", 6), ("spread", 1),
+    ("second", 4), ("first", 7), ("spread", 2), ("second", 5), ("keys", 0), ("spread", 3),
+    ("second", 6), ("keys", 1), ("spread", 4), ("second", 7), ("again", 0), ("keys", 2),
+    ("spread", 5), ("fold", 0, 1), ("again", 1), ("spread", 6), ("keys", 3), ("fold", 1, 3),
+    ("spread", 7), ("again", 2), ("keys", 4), ("fold", 2, 5), ("again", 3), ("keys", 5),
+    ("fold", 3, 3), ("keys", 6), ("again", 4), ("fold", 3, 4), ("fold", 4, 3), ("keys", 7),
+    ("again", 5), ("fold", 4, 6), ("fold", 5, 3), ("again", 6), ("fold", 5, 8), ("fold", 6, 3),
+    ("again", 7), ("fold", 6, 10), ("fold", 7, 15),
+)
 LOG2E = math.log2(math.e)
 LN2 = math.log(2.0)
 
@@ -46,12 +57,17 @@
     return out
 
 
-def route(pairs, group, x):
+def route(pairs, group):
     slots = []
+    images = []
     for pair in range(8):
         for side in range(2):
             image = pairs[group, side, pair]
-            slots.append((lax.rem(image // IMAGES - group + GROUPS, GROUPS), lax.rem(image, IMAGES)))
+            away = lax.rem(image // IMAGES - group + GROUPS, GROUPS)
+            for earlier in images:
+                away = jnp.where(image == earlier, 0, away)
+            images.append(image)
+            slots.append((away, lax.rem(image, IMAGES)))
     one = [[jnp.where(d == k, 1, 0) for d, _ in slots] for k in range(GROUPS)]
     near, far, behind = (sum(one[k]) for k in (1, 2, 3))
     least = jnp.maximum(jnp.maximum(far - RELAY, behind + far - ENTER), 0)
@@ -75,7 +91,7 @@
         )
         for k in range(1, GROUPS):
             rank[k] = rank[k] + one[k][s]
-    return routed, jnp.where(least > most, 1, 0)
+    return images, routed, jnp.where(least > most, 1, 0)
 
 
 def at_place(entries, k):
@@ -86,7 +102,7 @@
     return jnp.minimum(jnp.maximum(value, 0), count - 1)
 
 
-def kernel(scale, narrow, pairs, counts, desc, out, *scratch):
+def kernel(scale, narrow, pairs_in, counts_in, desc, out, *scratch):
     if narrow:
         misfit, scratch = scratch[0], scratch[1:]
         every_pair, relay_code, enter_code, slot_code = scratch[-4:]
@@ -103,8 +119,9 @@
     staged = scratch[CHUNKS : 2 * CHUNKS]
     (
         queries, keys, scores, row_top, row_sum, col_top, col_sum, key_bias, query_bias,
-        col_log, col_half, best_cols, held_even, held_odd, sent, got,
+        col_log, col_half, best_cols, turned, held_even, held_odd, sent, got,
         load_sem, xs, xr, qs, qr, ks, kr, fs, fr, cs, cr, os_, or_,
+        pairs, counts, small_sem,
     ) = scratch[2 * CHUNKS :]
     x, y, z, c = (lax.axis_index(a) for a in ("grp",) + TILE)
     right = (lax.rem(x + 1, 4), y, z, c)
@@ -126,6 +143,20 @@
     def peer_place(dy, dk):
         return lax.rem(y + dy, 4) * 2 + (half if dk == 0 else 1 - half)
 
+    others = [(dy, dk) for dy in range(4) for dk in range(2) if (dy, dk) != (0, 0)]
+    barrier = pltpu.get_barrier_semaphore()
+    greeted = [right, left, beside, sibling, diagonal] + [peer(dy, dk) for dy, dk in others]
+    if narrow:
+        greeted.append(opposite)
+    for device in greeted:
+        pl.semaphore_signal(barrier, inc=1, device_id=device, device_id_type=MESH)
+
+    small = [
+        pltpu.make_async_copy(pairs_in, pairs, small_sem.at[0]),
+        pltpu.make_async_copy(counts_in, counts, small_sem.at[1]),
+    ]
+    for copy in small:
+        copy.start()
     loads = [
         pltpu.make_async_copy(
             desc.at[:, pl.ds(r * ROWS, ROWS), :], gathered[r].at[pl.ds(0, IMAGES)], load_sem.at[r]
@@ -135,14 +166,8 @@
     for load in loads:
         load.start()
 
-    others = [(dy, dk) for dy in range(4) for dk in range(2) if (dy, dk) != (0, 0)]
-    barrier = pltpu.get_barrier_semaphore()
-    greeted = [right, left, beside, sibling, diagonal] + [peer(dy, dk) for dy, dk in others]
-    if narrow:
-        greeted.append(opposite)
-    for device in greeted:
-        pl.semaphore_signal(barrier, inc=1, device_id=device, device_id_type=MESH)
-
+    for copy in small:
+        copy.wait()
     p = place
     query_count = counts[pairs[0, p]]
     key_count = counts[pairs[1, p]]
@@ -268,18 +293,15 @@
         landed(block, fs.at[0, r], fr.at[0, r])
         go(remote(block, block, fs.at[2, r], fr.at[2, r], sibling))
 
-    def product(qi, kj, held):
+    def product(qi, kj):
         q = queries[qi].reshape(128, 256)
-        k = keys[kj].reshape(512, 256)
-        held[...] = lax.dot_general(
-            q, k, (((1,), (1,)), ((), ())), preferred_element_type=jnp.float32
-        )
+        return jnp.dot(q, turned[kj], preferred_element_type=jnp.float32)
 
     def fold(qi, kj, held):
         kb = key_bias[kj]
         top = col_top[kj]
+        high = top
         tops = []
-        high = top
         for g in range(8):
             rows = pl.ds(g * 16, 16)
             t = held[rows, :] * scale + kb
@@ -290,12 +312,11 @@
             )
             both = jnp.concatenate(parts, axis=1)
             scores[qi, kj, rows, :] = both
-            held[rows, :] = both
             high = jnp.maximum(high, jnp.maximum(both[:8], both[8:]))
         total = col_sum[kj] * jnp.exp2(top - high)
         for g in range(8):
             rows = pl.ds(g * 16, 16)
-            t = held[rows, :]
+            t = scores[qi, kj, rows, :]
             before = row_top[qi, rows, :]
             now = jnp.maximum(before, tops[g])
             acc = row_sum[qi, rows, :] * jnp.exp2(before - now)
@@ -307,25 +328,41 @@
         col_sum[kj] = total
         col_top[kj] = high
 
-    def first_pass(r):
+    def fold_tiles(at, count):
+        def ahead(n):
+            return product(*at(jnp.minimum(n, count - 1)))
+
+        def body(i, carry):
+            now, then = ahead(2 * i + 2), ahead(2 * i + 3)
+            fold(*at(2 * i), held_even)
+            fold(*at(2 * i + 1), held_odd)
+            held_even[...] = now
+            held_odd[...] = then
+            return carry
+
+        held_even[...] = ahead(0)
+        if count > 1:
+            held_odd[...] = ahead(1)
+            lax.fori_loop(0, count // 2, body, 0)
+        if count % 2:
+            fold(*at(count - 1), held_even)
+
+    def wait_chunk(r):
         for s in range(SOURCES):
             landed(queries.at[r, s], qs.at[r, 0], qr.at[r, s])
         landed(keys.at[r, parity * 2 + 1 - c], fs.at[1, r], fr.at[1, r])
         landed(keys.at[r, (1 - parity) * 2 + 1 - c], fs.at[2, r], fr.at[2, r])
+        turned[r] = jnp.transpose(keys[r].reshape(512, 256))
+
+    def first_pass(r, begin, count):
+        if begin == 0:
+            wait_chunk(r)
 
         def at(n):
+            n = n + begin
             return jnp.minimum(n, r), jnp.where(n <= r, r, n - r - 1)
 
-        def body(n, carry):
-            product(*at(2 * n + 1), held_odd)
-            fold(*at(2 * n), held_even)
-            product(*at(2 * n + 2), held_even)
-            fold(*at(2 * n + 1), held_odd)
-            return carry
-
-        product(*at(0), held_even)
-        lax.fori_loop(0, r, body, 0)
-        fold(*at(2 * r), held_even)
+        fold_tiles(at, count)
 
     def work_out_routes():
         for side in range(2):
@@ -335,20 +372,25 @@
             other = lax.rem(x + e, GROUPS)
             landed(every_pair.at[other], ps.at[e], pr.at[e])
         before, after, across = (lax.rem(x + k, GROUPS) for k in (3, 1, 2))
-        routed, bad = route(every_pair, x, x)
+        images, routed, bad = route(every_pair, x)
+        codes = []
         for s, (d, image, right_place, left_place, _, _) in enumerate(routed):
             far = jnp.where(
                 right_place >= 0, within(right_place, ENTER), ENTER + within(left_place, ENTER)
             )
-            slot_code[s] = jnp.where(d == 0, image, IMAGES + far)
-        routed, now = route(every_pair, before, x)
+            code = jnp.where(d == 0, image, IMAGES + far)
+            for earlier, same in zip(images, codes):
+                code = jnp.where(images[s] == earlier, same, code)
+            codes.append(code)
+            slot_code[s] = code
+        _, routed, now = route(every_pair, before)
         bad += now
         entries = [
             (p, jnp.where(d == 1, i, IMAGES + within(m, RELAY))) for d, i, p, _, m, _ in routed
         ]
         for k in range(ENTER):
             enter_code[k] = at_place(entries, k)
-        routed, now = route(every_pair, after, x)
+        _, routed, now = route(every_pair, after)
         bad += now
         entries = [
             (p, jnp.where(d == 3, i, IMAGES + RELAY + within(m, RELAY)))
@@ -356,7 +398,7 @@
         ]
         for k in range(ENTER):
             enter_code[ENTER + k] = at_place(entries, k)
-        routed, now = route(every_pair, across, x)
+        _, routed, now = route(every_pair, across)
         bad += now
         for k in range(RELAY):
             relay_code[k] = at_place([(m, i) for _, i, _, _, m, _ in routed], k)
@@ -369,21 +411,26 @@
     x_first(0)
     if narrow:
         work_out_routes()
-    x_first(1)
-    for i in range(CHUNKS + 4):
-        if i < CHUNKS:
-            x_second(i)
-            if i + 2 < CHUNKS:
-                x_first(i + 2)
-        if 0 <= i - 1 < CHUNKS:
-            select(i - 1)
-            spread(i - 1)
-        if 0 <= i - 2 < CHUNKS:
-            pass_keys(i - 2)
-        if 0 <= i - 3 < CHUNKS:
-            pass_again(i - 3)
-        if 0 <= i - 4 < CHUNKS:
-            first_pass(i - 4)
+    taken = [0] * CHUNKS
+    for step, r, *count in ORDER:
+        if step == "first":
+            x_first(r)
+        elif step == "second":
+            x_second(r)
+        elif step == "spread":
+            select(r)
+            spread(r)
+        elif step == "keys":
+            pass_keys(r)
+        elif step == "again":
+            pass_again(r)
+        elif narrow:
+            first_pass(r, taken[r], count[0])
+            taken[r] += count[0]
+    if not narrow:
+        for r in range(CHUNKS):
+            wait_chunk(r)
+        fold_tiles(lambda n: (n // CHUNKS, n % CHUNKS), CHUNKS * CHUNKS)
 
     for kj in range(CHUNKS):
         top = jnp.max(col_top[kj], axis=0, keepdims=True)
@@ -493,6 +540,7 @@
         pltpu.VMEM((MEMBERS, CHUNKS, 1, 512), f32),
         pltpu.VMEM((CHUNKS, 1, 512), f32),
         pltpu.VMEM((128, 128), f32),
+        pltpu.VMEM((CHUNKS, width, 512), bf16),
         pltpu.VMEM((128, 512), f32),
         pltpu.VMEM((128, 512), f32),
         pltpu.VMEM((8, 8, 128), f32),
@@ -504,6 +552,7 @@
         dma((3, CHUNKS)), dma((3, CHUNKS)),
         dma((4,)), dma((4,)),
         dma((8,)), dma((8,)),
+        pltpu.SMEM((2, 8), jnp.int32), pltpu.SMEM((64,), jnp.int32), dma((2,)),
     ]
     smem, vmem = pltpu.SMEM, pltpu.VMEM
 
@@ -526,8 +575,8 @@
             functools.partial(kernel, scale, narrow),
             out_shape=shapes[:count],
             in_specs=[
-                pl.BlockSpec(memory_space=smem),
-                pl.BlockSpec(memory_space=smem),
+                pl.BlockSpec(memory_space=pl.ANY),
+                pl.BlockSpec(memory_space=pl.ANY),
                 pl.BlockSpec(memory_space=pl.ANY),
             ],
             out_specs=[pl.BlockSpec(memory_space=vmem)] * count,

time: 75.6 us -> 66.7 us (0.88)
  Pallas kernels: 71.4 us -> 62.7 us
    pallas_call x1, Pallas kernels: 71.4 us -> 62.7 us  [call(): pl.pallas_call(functools.partial(kernel, scale, narrow), out_shape=shapes...]
where the time goes in v4:
time: 66.7 us; the launch traced here: 66.5 us
  Pallas kernels  62.7 us (94%)
  local copies, waits for them, and re-layouts  2.47 us (4%)
  between operations  1.32 us (2%)
    pallas_call x1, Pallas kernels, call(): pl.pallas_call(functools.partial(kernel, scale, narrow), out_shape=shapes...  62.7 us

profile of v4, /device:TPU:1, one launch (start us, length us, event | category | flops | bytes accessed | tf_op | source)
XLA Modules:
  0.0 66.5 jit_solution(4788039335585804913)
XLA Ops:
  0.6 0.0 copy-start
  0.6 0.0 copy-start.1
  0.7 0.7 copy-done
  1.3 0.0 copy-done.1
  1.3 62.7 %narrow.1 = (f32[3,8,128]{2,1,0:T(8,128)S(1)}, s32[8,128]{1,0:T(8,128)}) custom-call(s32[2,8]{1,0:T(2,128)S(1)} %bitcast.9, s32[64]{0:T(128)S(1)} %copy-done.1, bf16[16,128,256]{2,1,0:T(8,128)(2,1)} %desc.1), custom_call_target="tpu_custom_call" | custom-call | tf_op jit(solution)/shard_map/narrow/pallas_call | solution.py:574
  64.0 1.2 %slice.21 = s32[1,1]{1,0:T(1,128)} slice(s32[8,128]{1,0:T(8,128)} %get-tuple-element.15), slice={[0:1], [0:1]} | slice | bytes 8 | tf_op jit(solution)/shard_map/slice | solution.py:596
  65.9 0.6 slice_bitcast_fusion.2
  (1 shorter events, 0.0 us)
Async XLA Ops:
  0.6 0.7 %copy-start = (s32[8,2]{0,1:T(2,128)S(1)}, s32[8,2]{0,1:T(2,128)}, u32[]{:S(2)}) copy-start(s32[8,2]{0,1:T(2,128)} %param.6) | copy-start | bytes 196
  0.6 0.7 %copy-start.1 = (s32[64]{0:T(128)S(1)}, s32[64]{0:T(128)}, u32[]{:S(2)}) copy-start(s32[64]{0:T(128)} %counts_in.1) | copy-start | bytes 772

commit v5 on v4

--- a/solution.py
+++ b/solution.py
@@ -21,17 +21,17 @@
 MEMBERS = 4
 ENTER = 9
 RELAY = 4
-WIDE = 1
+WIDE = 2
 ORDER = (
-    ("first", 1), ("second", 0), ("first", 2), ("first", 3), ("second", 1), ("first", 4),
-    ("spread", 0), ("second", 2), ("first", 5), ("second", 3), ("first", 6), ("spread", 1),
-    ("second", 4), ("first", 7), ("spread", 2), ("second", 5), ("keys", 0), ("spread", 3),
-    ("second", 6), ("keys", 1), ("spread", 4), ("second", 7), ("again", 0), ("keys", 2),
-    ("spread", 5), ("fold", 0, 1), ("again", 1), ("spread", 6), ("keys", 3), ("fold", 1, 3),
-    ("spread", 7), ("again", 2), ("keys", 4), ("fold", 2, 5), ("again", 3), ("keys", 5),
-    ("fold", 3, 3), ("keys", 6), ("again", 4), ("fold", 3, 4), ("fold", 4, 3), ("keys", 7),
-    ("again", 5), ("fold", 4, 6), ("fold", 5, 3), ("again", 6), ("fold", 5, 8), ("fold", 6, 3),
-    ("again", 7), ("fold", 6, 10), ("fold", 7, 15),
+    ("second", 0), ("first", 2), ("first", 3), ("second", 1), ("first", 4), ("spread", 0),
+    ("second", 2), ("first", 5), ("second", 3), ("first", 6), ("spread", 1), ("second", 4),
+    ("first", 7), ("spread", 2), ("second", 5), ("keys", 0), ("spread", 3), ("second", 6),
+    ("keys", 1), ("spread", 4), ("second", 7), ("again", 0), ("keys", 2), ("spread", 5),
+    ("fold", 0, 1), ("spread", 6), ("keys", 3), ("again", 1), ("spread", 7), ("again", 2),
+    ("keys", 4), ("fold", 1, 3), ("fold", 2, 2), ("again", 3), ("keys", 5), ("fold", 2, 3),
+    ("fold", 3, 2), ("keys", 6), ("again", 4), ("fold", 3, 5), ("fold", 4, 2), ("keys", 7),
+    ("again", 5), ("fold", 4, 7), ("fold", 5, 2), ("again", 6), ("fold", 5, 9), ("fold", 6, 2),
+    ("again", 7), ("fold", 6, 11), ("fold", 7, 15),
 )
 LOG2E = math.log2(math.e)
 LN2 = math.log(2.0)
@@ -328,9 +328,9 @@
         col_sum[kj] = total
         col_top[kj] = high
 
-    def fold_tiles(at, count):
+    def fold_tiles(at, begin, end, last):
         def ahead(n):
-            return product(*at(jnp.minimum(n, count - 1)))
+            return product(*at(jnp.minimum(n, last - 1)))
 
         def body(i, carry):
             now, then = ahead(2 * i + 2), ahead(2 * i + 3)
@@ -340,12 +340,12 @@
             held_odd[...] = then
             return carry
 
-        held_even[...] = ahead(0)
-        if count > 1:
+        if begin == 0:
+            held_even[...] = ahead(0)
             held_odd[...] = ahead(1)
-            lax.fori_loop(0, count // 2, body, 0)
-        if count % 2:
-            fold(*at(count - 1), held_even)
+        lax.fori_loop(begin // 2, end // 2, body, 0)
+        if end % 2:
+            fold(*at(end - 1), held_even)
 
     def wait_chunk(r):
         for s in range(SOURCES):
@@ -359,10 +359,9 @@
             wait_chunk(r)
 
         def at(n):
-            n = n + begin
             return jnp.minimum(n, r), jnp.where(n <= r, r, n - r - 1)
 
-        fold_tiles(at, count)
+        fold_tiles(at, begin, begin + count, 2 * r + 1)
 
     def work_out_routes():
         for side in range(2):
@@ -408,7 +407,8 @@
     if narrow:
         for e, device in ((3, right), (1, left), (2, opposite)):
             go(remote(pairs, every_pair.at[x], ps.at[e], pr.at[e], device))
-    x_first(0)
+    for r in range(WIDE):
+        x_first(r)
     if narrow:
         work_out_routes()
     taken = [0] * CHUNKS
@@ -430,12 +430,14 @@
     if not narrow:
         for r in range(CHUNKS):
             wait_chunk(r)
-        fold_tiles(lambda n: (n // CHUNKS, n % CHUNKS), CHUNKS * CHUNKS)
+        fold_tiles(lambda n: (n // CHUNKS, n % CHUNKS), 0, CHUNKS**2, CHUNKS**2)
 
     for kj in range(CHUNKS):
         top = jnp.max(col_top[kj], axis=0, keepdims=True)
         total = jnp.sum(col_sum[kj] * jnp.exp2(col_top[kj] - top), axis=0, keepdims=True)
-        col_log[member, kj] = top + jnp.log2(total)
+        log = top + jnp.log2(total)
+        for m in range(MEMBERS):
+            col_log[member, m, pl.ds(kj, 1), :] = log[:, m * 128 : (m + 1) * 128]
     team = [(1, sibling), (2, beside), (3, diagonal)]
 
     def mate(e):
@@ -455,27 +457,21 @@
 
     for e, _ in team:
         landed(col_log.at[mate(e)], cs.at[e], cr.at[e])
-    cols = []
-    for kj in range(CHUNKS):
-        logs = [col_log[m, kj] for m in range(MEMBERS)]
+    own_col = None
+    for m in range(MEMBERS):
+        logs = [col_log[k, m] for k in range(MEMBERS)]
         top = jnp.maximum(jnp.maximum(logs[0], logs[1]), jnp.maximum(logs[2], logs[3]))
-        total = sum(jnp.exp2(v - top) for v in logs)
-        full = top + jnp.log2(total)
-        col_half[kj] = full * 0.5
-        mine = full[:, :128]
-        for m in range(1, MEMBERS):
-            mine = jnp.where(member == m, full[:, m * 128 : (m + 1) * 128], mine)
-        cols.append(mine)
-    own_col = jnp.concatenate(cols, axis=0)
+        full = top + jnp.log2(sum(jnp.exp2(v - top) for v in logs))
+        col_half[m] = full * 0.5
+        own_col = full if m == 0 else jnp.where(member == m, full, own_col)
 
     def second(qi, carry):
         best = [None] * 8
         for kj in range(CHUNKS):
-            half_log = col_half[kj]
+            halves = [col_half[m, pl.ds(kj, 1), :] for m in range(MEMBERS)]
             for g in range(8):
                 t = scores[qi, kj, pl.ds(g * 16, 16), :]
-                t = t - half_log
-                parts = [t[:, m * 128 : (m + 1) * 128] for m in range(MEMBERS)]
+                parts = [t[:, m * 128 : (m + 1) * 128] - halves[m] for m in range(MEMBERS)]
                 part = jnp.maximum(
                     jnp.maximum(parts[0], parts[1]), jnp.maximum(parts[2], parts[3])
                 )
@@ -537,8 +533,8 @@
         pltpu.VMEM((CHUNKS, 8, 512), f32),
         pltpu.VMEM((CHUNKS, 1, 512), f32),
         pltpu.VMEM((CHUNKS, 128, 128), f32),
-        pltpu.VMEM((MEMBERS, CHUNKS, 1, 512), f32),
-        pltpu.VMEM((CHUNKS, 1, 512), f32),
+        pltpu.VMEM((MEMBERS, MEMBERS, CHUNKS, 128), f32),
+        pltpu.VMEM((MEMBERS, CHUNKS, 128), f32),
         pltpu.VMEM((128, 128), f32),
         pltpu.VMEM((CHUNKS, width, 512), bf16),
         pltpu.VMEM((128, 512), f32),
@@ -569,7 +565,7 @@
                 smem((2 * ENTER,), jnp.int32),
                 smem((IMAGES,), jnp.int32),
             ]
-        shapes = [jax.ShapeDtypeStruct((3, 8, 128), f32), jax.ShapeDtypeStruct((8, 128), jnp.int32)]
+        shapes = [jax.ShapeDtypeStruct((3, 8, 128), f32), jax.ShapeDtypeStruct((1, 1), jnp.int32)]
         count = 2 if narrow else 1
         return pl.pallas_call(
             functools.partial(kernel, scale, narrow),
@@ -593,7 +589,7 @@
         return out[0], out[1], out[2]
 
     out, misfit = call(True)
-    return lax.cond(misfit[0, 0] > 0, lambda _: split(call(False)[0]), split, out)
+    return lax.cond(misfit.reshape(()) > 0, lambda _: split(call(False)[0]), split, out)
 
 
 def solution(mesh):

time: 66.7 us -> 64.4 us (0.966)
  local copies, waits for them, and re-layouts: 2.47 us -> 1.27 us
  Pallas kernels: 62.7 us -> 61.8 us
    slice x1 -> x0, local copies, waits for them, and re-layouts: 1.2 us -> none  [local(): misfit[0, 0] > 0]
    pallas_call x1, Pallas kernels: 62.7 us -> 61.8 us  [call(): pl.pallas_call(functools.partial(kernel, scale, narrow), out_shape=shapes...]
where the time goes in v5:
time: 64.4 us; the launch traced here: 64.3 us
  Pallas kernels  61.8 us (96%)
  local copies, waits for them, and re-layouts  1.27 us (2%)
  between operations  1.22 us (2%)
    pallas_call x1, Pallas kernels, call(): pl.pallas_call(functools.partial(kernel, scale, narrow), out_shape=shapes...  61.8 us

profile of v5, /device:TPU:1, one launch (start us, length us, event | category | flops | bytes accessed | tf_op | source)
XLA Modules:
  0.0 64.3 jit_solution(8100536010013371337)
XLA Ops:
  0.6 0.0 copy-start
  0.6 0.0 copy-start.1
  0.7 0.7 %copy-done = s32[8,2]{0,1:T(2,128)S(1)} copy-done((s32[8,2]{0,1:T(2,128)S(1)}, s32[8,2]{0,1:T(2,128)}, u32[]{:S(2)}) %copy-start) | copy-done | bytes 88
  1.3 0.0 copy-done.1
  1.3 61.8 %narrow.1 = (f32[3,8,128]{2,1,0:T(8,128)S(1)}, s32[1,1]{1,0:T(1,128)}) custom-call(s32[2,8]{1,0:T(2,128)S(1)} %bitcast.9, s32[64]{0:T(128)S(1)} %copy-done.1, bf16[16,128,256]{2,1,0:T(8,128)(2,1)} %desc.1), custom_call_target="tpu_custom_call" | custom-call | tf_op jit(solution)/shard_map/narrow/pallas_call | solution.py:570
  63.7 0.6 slice_bitcast_fusion.2
  (1 shorter events, 0.0 us)
Async XLA Ops:
  0.6 0.7 %copy-start = (s32[8,2]{0,1:T(2,128)S(1)}, s32[8,2]{0,1:T(2,128)}, u32[]{:S(2)}) copy-start(s32[8,2]{0,1:T(2,128)} %param.6) | copy-start | bytes 196
  0.6 0.7 %copy-start.1 = (s32[64]{0:T(128)S(1)}, s32[64]{0:T(128)}, u32[]{:S(2)}) copy-start(s32[64]{0:T(128)} %counts_in.1) | copy-start | bytes 772

commit v6 on v5

--- a/solution.py
+++ b/solution.py
@@ -27,11 +27,12 @@
     ("second", 2), ("first", 5), ("second", 3), ("first", 6), ("spread", 1), ("second", 4),
     ("first", 7), ("spread", 2), ("second", 5), ("keys", 0), ("spread", 3), ("second", 6),
     ("keys", 1), ("spread", 4), ("second", 7), ("again", 0), ("keys", 2), ("spread", 5),
-    ("fold", 0, 1), ("spread", 6), ("keys", 3), ("again", 1), ("spread", 7), ("again", 2),
-    ("keys", 4), ("fold", 1, 3), ("fold", 2, 2), ("again", 3), ("keys", 5), ("fold", 2, 3),
-    ("fold", 3, 2), ("keys", 6), ("again", 4), ("fold", 3, 5), ("fold", 4, 2), ("keys", 7),
-    ("again", 5), ("fold", 4, 7), ("fold", 5, 2), ("again", 6), ("fold", 5, 9), ("fold", 6, 2),
-    ("again", 7), ("fold", 6, 11), ("fold", 7, 15),
+    ("columns", 0, 1), ("rows", 1, 1), ("spread", 6), ("again", 1), ("keys", 3), ("spread", 7),
+    ("columns", 1, 2), ("again", 2), ("keys", 4), ("rows", 2, 2), ("columns", 2, 3), ("keys", 5),
+    ("again", 3), ("rows", 3, 3), ("columns", 3, 2), ("again", 4), ("keys", 6), ("columns", 3, 2),
+    ("rows", 4, 4), ("columns", 4, 2), ("again", 5), ("keys", 7), ("columns", 4, 3),
+    ("rows", 5, 5), ("columns", 5, 2), ("again", 6), ("columns", 5, 4), ("rows", 6, 4),
+    ("rows", 6, 2), ("again", 7), ("columns", 6, 7), ("rows", 7, 7), ("columns", 7, 8),
 )
 LOG2E = math.log2(math.e)
 LN2 = math.log(2.0)
@@ -119,7 +120,7 @@
     staged = scratch[CHUNKS : 2 * CHUNKS]
     (
         queries, keys, scores, row_top, row_sum, col_top, col_sum, key_bias, query_bias,
-        col_log, col_half, best_cols, turned, held_even, held_odd, sent, got,
+        col_log, col_half, best_lanes, turned, held_even, held_odd, sent, got,
         load_sem, xs, xr, qs, qr, ks, kr, fs, fr, cs, cr, os_, or_,
         pairs, counts, small_sem,
     ) = scratch[2 * CHUNKS :]
@@ -347,21 +348,26 @@
         if end % 2:
             fold(*at(end - 1), held_even)
 
-    def wait_chunk(r):
+    def wait_rows(r):
         for s in range(SOURCES):
             landed(queries.at[r, s], qs.at[r, 0], qr.at[r, s])
+
+    def wait_columns(r):
         landed(keys.at[r, parity * 2 + 1 - c], fs.at[1, r], fr.at[1, r])
         landed(keys.at[r, (1 - parity) * 2 + 1 - c], fs.at[2, r], fr.at[2, r])
         turned[r] = jnp.transpose(keys[r].reshape(512, 256))
 
-    def first_pass(r, begin, count):
+    def fold_rows(r, begin, count):
         if begin == 0:
-            wait_chunk(r)
-
-        def at(n):
-            return jnp.minimum(n, r), jnp.where(n <= r, r, n - r - 1)
-
-        fold_tiles(at, begin, begin + count, 2 * r + 1)
+            wait_rows(r)
+        fold_tiles(lambda n: (r, n), begin, begin + count, r)
+
+    def fold_columns(r, begin, count):
+        if begin == 0:
+            if r == 0:
+                wait_rows(r)
+            wait_columns(r)
+        fold_tiles(lambda n: (n, r), begin, begin + count, r + 1)
 
     def work_out_routes():
         for side in range(2):
@@ -411,7 +417,7 @@
         x_first(r)
     if narrow:
         work_out_routes()
-    taken = [0] * CHUNKS
+    taken = {"rows": [0] * CHUNKS, "columns": [0] * CHUNKS}
     for step, r, *count in ORDER:
         if step == "first":
             x_first(r)
@@ -425,11 +431,12 @@
         elif step == "again":
             pass_again(r)
         elif narrow:
-            first_pass(r, taken[r], count[0])
-            taken[r] += count[0]
+            (fold_rows if step == "rows" else fold_columns)(r, taken[step][r], count[0])
+            taken[step][r] += count[0]
     if not narrow:
         for r in range(CHUNKS):
-            wait_chunk(r)
+            wait_rows(r)
+            wait_columns(r)
         fold_tiles(lambda n: (n // CHUNKS, n % CHUNKS), 0, CHUNKS**2, CHUNKS**2)
 
     for kj in range(CHUNKS):
@@ -477,14 +484,15 @@
                 )
                 best[g] = part if kj == 0 else jnp.maximum(best[g], part)
         for g in range(8):
-            rows = pl.ds(g * 16, 16)
-            most = jnp.max(best[g], axis=1, keepdims=True)
-            best_cols[rows, :] = jnp.where(lane[:16] == qi, most, best_cols[rows, :])
+            best_lanes[qi, pl.ds(g * 16, 16), :] = best[g]
         return carry
 
-    best_cols[...] = jnp.zeros((128, 128), jnp.float32)
     lax.fori_loop(0, CHUNKS, second, 0)
-    best = 2.0 * jnp.transpose(best_cols[...])[:8] - row_log
+    best_cols = jnp.zeros((128, 128), jnp.float32)
+    for qi in range(CHUNKS):
+        most = jnp.max(best_lanes[qi], axis=1, keepdims=True)
+        best_cols = jnp.where(lane == qi, most, best_cols)
+    best = 2.0 * jnp.transpose(best_cols)[:8] - row_log
 
     chunk = lax.broadcasted_iota(jnp.int32, (8, 128), 0)
     lane8 = lax.broadcasted_iota(jnp.int32, (8, 128), 1)
@@ -499,6 +507,7 @@
         value = block_transpose(value)
         for s in range(SOURCES):
             sent[s, pl.ds(j, 1), :] = value[s : s + 1]
+    before = len(started)
     for dy in range(4):
         for dk in range(2):
             e = dy * 2 + dk
@@ -507,12 +516,14 @@
                 pltpu.make_async_copy(sent.at[to], got.at[place], or_.at[place]).start()
             else:
                 go(remote(sent.at[to], got.at[place], os_.at[e], or_.at[place], peer(dy, dk)))
+    for copy in started[:before]:
+        copy.wait_send()
     for s in range(SOURCES):
         landed(got.at[s], os_.at[0], or_.at[s])
     for s in range(SOURCES):
         for j in range(3):
             out[j, pl.ds(s, 1), :] = got[s, pl.ds(j, 1), :]
-    for copy in started:
+    for copy in started[before:]:
         copy.wait_send()
 
 
@@ -535,7 +546,7 @@
         pltpu.VMEM((CHUNKS, 128, 128), f32),
         pltpu.VMEM((MEMBERS, MEMBERS, CHUNKS, 128), f32),
         pltpu.VMEM((MEMBERS, CHUNKS, 128), f32),
-        pltpu.VMEM((128, 128), f32),
+        pltpu.VMEM((CHUNKS, 128, 128), f32),
         pltpu.VMEM((CHUNKS, width, 512), bf16),
         pltpu.VMEM((128, 512), f32),
         pltpu.VMEM((128, 512), f32),

time: 64.4 us -> 63.6 us (0.988)
  Pallas kernels: 61.8 us -> 61 us
    pallas_call x1, Pallas kernels: 61.8 us -> 61 us  [call(): pl.pallas_call(functools.partial(kernel, scale, narrow), out_shape=shapes...]
where the time goes in v6:
time: 63.6 us; the launch traced here: 63.5 us
  Pallas kernels  61 us (96%)
  local copies, waits for them, and re-layouts  1.27 us (2%)
  between operations  1.22 us (2%)
    pallas_call x1, Pallas kernels, call(): pl.pallas_call(functools.partial(kernel, scale, narrow), out_shape=shapes...  61 us

profile of v6, /device:TPU:1, one launch (start us, length us, event | category | flops | bytes accessed | tf_op | source)
XLA Modules:
  0.0 63.5 jit_solution(17051349357879705854)
XLA Ops:
  0.6 0.0 copy-start
  0.6 0.0 copy-start.1
  0.7 0.7 %copy-done = s32[8,2]{0,1:T(2,128)S(1)} copy-done((s32[8,2]{0,1:T(2,128)S(1)}, s32[8,2]{0,1:T(2,128)}, u32[]{:S(2)}) %copy-start) | copy-done | bytes 88
  1.3 0.0 copy-done.1
  1.3 61.0 %narrow.1 = (f32[3,8,128]{2,1,0:T(8,128)S(1)}, s32[1,1]{1,0:T(1,128)}) custom-call(s32[2,8]{1,0:T(2,128)S(1)} %bitcast.9, s32[64]{0:T(128)S(1)} %copy-done.1, bf16[16,128,256]{2,1,0:T(8,128)(2,1)} %desc.1), custom_call_target="tpu_custom_call" | custom-call | tf_op jit(solution)/shard_map/narrow/pallas_call | solution.py:581
  62.9 0.6 slice_bitcast_fusion.2
  (1 shorter events, 0.0 us)
Async XLA Ops:
  0.6 0.7 %copy-start = (s32[8,2]{0,1:T(2,128)S(1)}, s32[8,2]{0,1:T(2,128)}, u32[]{:S(2)}) copy-start(s32[8,2]{0,1:T(2,128)} %param.6) | copy-start | bytes 196
  0.6 0.7 %copy-start.1 = (s32[64]{0:T(128)S(1)}, s32[64]{0:T(128)}, u32[]{:S(2)}) copy-start(s32[64]{0:T(128)} %counts_in.1) | copy-start | bytes 772

commit v7 on v6

--- a/solution.py
+++ b/solution.py
@@ -27,12 +27,11 @@
     ("second", 2), ("first", 5), ("second", 3), ("first", 6), ("spread", 1), ("second", 4),
     ("first", 7), ("spread", 2), ("second", 5), ("keys", 0), ("spread", 3), ("second", 6),
     ("keys", 1), ("spread", 4), ("second", 7), ("again", 0), ("keys", 2), ("spread", 5),
-    ("columns", 0, 1), ("rows", 1, 1), ("spread", 6), ("again", 1), ("keys", 3), ("spread", 7),
-    ("columns", 1, 2), ("again", 2), ("keys", 4), ("rows", 2, 2), ("columns", 2, 3), ("keys", 5),
-    ("again", 3), ("rows", 3, 3), ("columns", 3, 2), ("again", 4), ("keys", 6), ("columns", 3, 2),
-    ("rows", 4, 4), ("columns", 4, 2), ("again", 5), ("keys", 7), ("columns", 4, 3),
-    ("rows", 5, 5), ("columns", 5, 2), ("again", 6), ("columns", 5, 4), ("rows", 6, 4),
-    ("rows", 6, 2), ("again", 7), ("columns", 6, 7), ("rows", 7, 7), ("columns", 7, 8),
+    ("fold", 0, 2), ("spread", 6), ("keys", 3), ("again", 1), ("spread", 7), ("fold", 1, 2),
+    ("keys", 4), ("again", 2), ("fold", 1, 2), ("fold", 2, 2), ("keys", 5), ("again", 3),
+    ("fold", 2, 4), ("fold", 3, 2), ("keys", 6), ("again", 4), ("fold", 3, 6), ("fold", 4, 2),
+    ("keys", 7), ("again", 5), ("fold", 4, 8), ("fold", 5, 2), ("again", 6), ("fold", 5, 10),
+    ("fold", 6, 2), ("again", 7), ("fold", 6, 12), ("fold", 7, 8),
 )
 LOG2E = math.log2(math.e)
 LN2 = math.log(2.0)
@@ -357,17 +356,19 @@
         landed(keys.at[r, (1 - parity) * 2 + 1 - c], fs.at[2, r], fr.at[2, r])
         turned[r] = jnp.transpose(keys[r].reshape(512, 256))
 
-    def fold_rows(r, begin, count):
-        if begin == 0:
-            wait_rows(r)
-        fold_tiles(lambda n: (r, n), begin, begin + count, r)
-
-    def fold_columns(r, begin, count):
+    def fold_chunk(r, begin, count):
+        final = r == CHUNKS - 1
         if begin == 0:
             if r == 0:
                 wait_rows(r)
             wait_columns(r)
-        fold_tiles(lambda n: (n, r), begin, begin + count, r + 1)
+            if not final:
+                wait_rows(r + 1)
+
+        def at(n):
+            return jnp.where(n <= r, n, r + 1), jnp.where(n <= r, r, n - r - 1)
+
+        fold_tiles(at, begin, begin + count, r + 1 if final else 2 * r + 2)
 
     def work_out_routes():
         for side in range(2):
@@ -417,7 +418,7 @@
         x_first(r)
     if narrow:
         work_out_routes()
-    taken = {"rows": [0] * CHUNKS, "columns": [0] * CHUNKS}
+    taken = [0] * CHUNKS
     for step, r, *count in ORDER:
         if step == "first":
             x_first(r)
@@ -431,8 +432,8 @@
         elif step == "again":
             pass_again(r)
         elif narrow:
-            (fold_rows if step == "rows" else fold_columns)(r, taken[step][r], count[0])
-            taken[step][r] += count[0]
+            fold_chunk(r, taken[r], count[0])
+            taken[r] += count[0]
     if not narrow:
         for r in range(CHUNKS):
             wait_rows(r)

time: 63.6 us -> 63.1 us (level)
  no operation moved by 1% of the time
where the time goes in v7:
time: 63.1 us; the launch traced here: 63 us
  Pallas kernels  60.5 us (96%)
  local copies, waits for them, and re-layouts  1.27 us (2%)
  between operations  1.22 us (2%)
    pallas_call x1, Pallas kernels, call(): pl.pallas_call(functools.partial(kernel, scale, narrow), out_shape=shapes...  60.5 us

profile of v7, /device:TPU:1, one launch (start us, length us, event | category | flops | bytes accessed | tf_op | source)
XLA Modules:
  0.0 63.0 jit_solution(12647630520844014906)
XLA Ops:
  0.6 0.0 copy-start
  0.6 0.0 copy-start.1
  0.7 0.7 %copy-done = s32[8,2]{0,1:T(2,128)S(1)} copy-done((s32[8,2]{0,1:T(2,128)S(1)}, s32[8,2]{0,1:T(2,128)}, u32[]{:S(2)}) %copy-start) | copy-done | bytes 88
  1.3 0.0 copy-done.1
  1.3 60.5 %narrow.1 = (f32[3,8,128]{2,1,0:T(8,128)S(1)}, s32[1,1]{1,0:T(1,128)}) custom-call(s32[2,8]{1,0:T(2,128)S(1)} %bitcast.9, s32[64]{0:T(128)S(1)} %copy-done.1, bf16[16,128,256]{2,1,0:T(8,128)(2,1)} %desc.1), custom_call_target="tpu_custom_call" | custom-call | tf_op jit(solution)/shard_map/narrow/pallas_call | solution.py:582
  62.4 0.6 slice_bitcast_fusion.2
  (1 shorter events, 0.0 us)
Async XLA Ops:
  0.6 0.7 %copy-start = (s32[8,2]{0,1:T(2,128)S(1)}, s32[8,2]{0,1:T(2,128)}, u32[]{:S(2)}) copy-start(s32[8,2]{0,1:T(2,128)} %param.6) | copy-start | bytes 196
  0.6 0.7 %copy-start.1 = (s32[64]{0:T(128)S(1)}, s32[64]{0:T(128)}, u32[]{:S(2)}) copy-start(s32[64]{0:T(128)} %counts_in.1) | copy-start | bytes 772
